TPU v7x, 32 devices: a whole 2x2x4 slice. The times are simulated.
32 devices in a mesh: gx: 4 (over z), gy: 4 (over x, core), gz: 2 (over y).
Axes of the slice: x: 2, y: 2, z: 4, core: 2. Of those that a mesh axis runs over, the one named last changes fastest.
Arguments:
- right_side: float32 [256, 256, 512], P('gx', 'gy', 'gz'), may hold values from -6 to 6
- guess: float32 [256, 256, 512], P('gx', 'gy', 'gz'), may hold values from -4 to 4
Outputs:
- updated: float32 [256, 256, 512], P('gx', 'gy', 'gz')
- new_residual: float32 [256, 256, 512], P('gx', 'gy', 'gz')
- res_norm: float32 [], replicated
All inputs are finite; a program needn't handle non-finite values.
Results may differ from a plain program's by a relative error of at most 0.0003.
Values sent between devices are 32-bit elements; how exact they have to be, the bound alone decides.
A program may use at most 128 MiB of HBM per device.

v0:
```python
import math

import jax
import jax.numpy as jnp
from jax import lax
from jax.sharding import PartitionSpec as P

COARSEN = 4


screen = 0.002
exact_prec = lax.Precision.HIGHEST


def padded_2(cells, sides, width):
    for axis, dim in sides:
        count = lax.axis_size(axis)
        head = lax.slice_in_dim(cells, 0, width, axis=dim)
        tail = lax.slice_in_dim(cells, cells.shape[dim] - width, cells.shape[dim], axis=dim)
        cells = jnp.concatenate(
            [
                lax.ppermute(tail, axis, [(i, (i + 1) % count) for i in range(count)]),
                cells,
                lax.ppermute(head, axis, [((i + 1) % count, i) for i in range(count)]),
            ],
            axis=dim,
        )
    return cells


def neighbours(padded):
    total = padded[2:, 1:-1, 1:-1] + padded[:-2, 1:-1, 1:-1]
    total = total + padded[1:-1, 2:, 1:-1] + padded[1:-1, :-2, 1:-1]
    total = total + padded[1:-1, 1:-1, 2:] + padded[1:-1, 1:-1, :-2]
    return total


def hartley(length):
    index = jnp.arange(length, dtype=jnp.int32)
    product = index[:, None] * index[None, :] % length
    angle = 2.0 * math.pi * product.astype(jnp.float32) / length
    return jnp.cos(angle) + jnp.sin(angle)


def eigen_line(index, length):
    phase = (index % length).astype(jnp.float32)
    return (2.0 - 2.0 * jnp.cos(2.0 * math.pi * phase / length)) / (COARSEN * COARSEN)


def along_first(values, matrix):
    return jnp.einsum("jab,jk->kab", values, matrix, precision=exact_prec)


def along_second(values, matrix):
    return jnp.einsum("ajb,jk->akb", values, matrix, precision=exact_prec)


def along_third(values, matrix):
    return jnp.einsum("abj,jk->abk", values, matrix, precision=exact_prec)


def fold_table(fine, coarse_len):
    fine_index = jnp.arange(fine, dtype=jnp.int32) // COARSEN
    coarse_index = jnp.arange(coarse_len, dtype=jnp.int32)
    return (fine_index[:, None] == coarse_index[None, :]).astype(jnp.float32)


def per_device(right_side, guess):
    diag_value = 6.0 + screen
    padded = padded_2(guess, (("gx", 0), ("gy", 1), ("gz", 2)), 1)
    residual_now = right_side - (diag_value * guess - neighbours(padded))
    first_sweep = residual_now / diag_value
    padded_sweep = padded_2(first_sweep, (("gx", 0), ("gy", 1), ("gz", 2)), 1)
    local_fix = (residual_now + neighbours(padded_sweep)) / diag_value
    block_x, block_y, block_z = guess.shape
    coarse_x = block_x // COARSEN
    coarse_y = block_y // COARSEN
    coarse_z = block_z // COARSEN
    fold_z = fold_table(block_z, coarse_z)
    planes = residual_now.reshape(coarse_x, COARSEN, coarse_y, COARSEN, block_z).sum(axis=(1, 3))
    coarse = along_third(planes, fold_z) / (COARSEN * COARSEN * COARSEN)
    length_x = coarse_x * lax.axis_size("gx")
    length_y = coarse_y * lax.axis_size("gy")
    length_z = coarse_z * lax.axis_size("gz")
    scale = 1.0 / (length_x * length_y * length_z)
    table_x = hartley(length_x)
    table_y = hartley(length_y)
    table_z = hartley(length_z)
    spectra = lax.all_to_all(coarse, "gz", split_axis=0, concat_axis=2, tiled=True)
    spectra = along_third(spectra, table_z)
    spectra = lax.all_to_all(spectra, "gy", split_axis=2, concat_axis=1, tiled=True)
    spectra = along_second(spectra, table_y)
    spectra = lax.all_to_all(spectra, ("gx", "gz"), split_axis=1, concat_axis=0, tiled=True)
    spectra = along_first(spectra, table_x)
    width_y = spectra.shape[1]
    width_z = spectra.shape[2]
    index_x = jnp.arange(length_x, dtype=jnp.int32)
    index_y = (
        lax.axis_index("gx") * lax.axis_size("gz") + lax.axis_index("gz")
    ) * width_y + jnp.arange(width_y, dtype=jnp.int32)
    index_z = lax.axis_index("gy") * width_z + jnp.arange(width_z, dtype=jnp.int32)
    eigen_sum = (
        screen
        + eigen_line(index_x, length_x)[:, None, None]
        + eigen_line(index_y, length_y)[None, :, None]
        + eigen_line(index_z, length_z)[None, None, :]
    )
    spectra = along_first(spectra / eigen_sum, table_x) * scale
    spectra = lax.all_to_all(spectra, ("gx", "gz"), split_axis=0, concat_axis=1, tiled=True)
    spectra = along_second(spectra, table_y)
    spectra = lax.all_to_all(spectra, "gy", split_axis=1, concat_axis=2, tiled=True)
    spectra = along_third(spectra, table_z)
    correction = lax.all_to_all(spectra, "gz", split_axis=2, concat_axis=0, tiled=True)
    spread = jnp.einsum("abk,jk->abj", correction, fold_z, precision=exact_prec)
    prolonged = jnp.broadcast_to(
        spread[:, None, :, None, :], (coarse_x, COARSEN, coarse_y, COARSEN, block_z)
    ).reshape(block_x, block_y, block_z)
    updated = guess + local_fix + prolonged
    padded_new = padded_2(updated, (("gx", 0), ("gy", 1), ("gz", 2)), 1)
    new_residual = right_side - (diag_value * updated - neighbours(padded_new))
    total = lax.psum(jnp.sum(new_residual * new_residual), ("gx", "gy", "gz"))
    return (updated, new_residual, jnp.sqrt(total))


def solution(mesh):
    return jax.shard_map(
        per_device,
        mesh=mesh,
        in_specs=(P("gx", "gy", "gz"), P("gx", "gy", "gz")),
        out_specs=(P("gx", "gy", "gz"), P("gx", "gy", "gz"), P()),
        check_vma=False,
    )
```

profile of v0, /device:TPU:0, one launch (start us, length us, event | category | flops | bytes accessed | tf_op | source)
XLA Modules:
  0.0 282.0 jit_solution(7367080916076902201)
XLA Ops:
  0.6 0.9 fusion.103
  1.6 5.1 %collective-permute-start = (f32[1,64,256]{2,0,1:T(1,128)S(1)}, f32[1,64,256]{2,0,1:T(1,128)S(1)}, u32[]{:S(2)}, u32[]{:S(2)}) collective-permute-start(f32[1,64,256]{2,0,1:T(1,128)S(1)} %copy.62), channel_id=1, source_target_pairs={{8,0},{16,8},{24,16},{0,24},{9,1},{17,9},{25,17},{1,25},{10,2},{18... | collective-permute-start | bytes 196616 | tf_op jit(solution)/shard_map/ppermute | solution.py:24
  6.9 6.6 %copy.76 = f32[64,64,256]{2,0,1:T(8,128)} copy(f32[64,64,256]{2,1,0:T(8,128)} %param.3) | data formatting | bytes 8388608 | tf_op args[1]
  13.5 1.0 pad_maximum_fusion.63
  15.6 1.6 collective-permute-done.2
  17.3 2.1 collective-permute-done.3
  20.1 2.2 fusion.100
  22.3 2.6 copy.67
  24.9 1.6 collective-permute-start.4
  26.5 0.9 copy.69
  28.0 1.2 collective-permute-done.4
  29.2 1.0 copy.68
  30.1 1.2 collective-permute-done.5
  31.4 2.4 copy.70
  33.8 24.9 %broadcast_multiply_fusion = (f32[64,64,256]{2,0,1:T(8,128)}, f32[64,64,256]{2,0,1:T(8,128)}) fusion(f32[66,1,256]{2,0,1:T(8,128)S(1)} %collective-permute-done.2, f32[1,64,256]{2,0,1:T(1,128)S(1)} %collective-permute-done, f32[64,64,256]{2,0,1:T(8,128)} %copy.76, f32[1,64,256]{2,0,1:T(1,128)S(1)} %collective-permute-done.1, ...), kind=kLoop, calls=%fused_computation.81 | loop fusion | flops 28311552 | bytes 17078304 | tf_op jit(solution)/shard_map/div | solution.py:72
  58.7 5.2 %reshape.117 = f32[16,4,16,4,256]{4,1,0,3,2:T(4,128)} reshape(f32[64,64,256]{2,0,1:T(8,128)} %get-tuple-element.12) | data formatting | bytes 8388608 | tf_op jit(solution)/shard_map/reshape | solution.py:80
  63.8 3.5 %reduce_sum.18 = f32[16,16,256]{2,0,1:T(8,128)S(1)} reduce(f32[16,4,16,4,256]{4,1,0,3,2:T(4,128)} %reshape.117, f32[]{:T(128)} %constant.120.clone.1), dimensions={1,3}, to_apply=%region_0.1 | reduce | flops 983040 | bytes 4456452 | tf_op jit(solution)/shard_map/reduce_sum | solution.py:80
  68.5 3.3 %all-to-all-start = ((f32[2,1,8192]{2,1,0:T(1,128)}), f32[2,1,8192]{2,1,0:T(1,128)S(1)}, u32[]{:S(2)}, u32[]{:S(2)}) async-start(f32[2,1,8192]{2,1,0:T(1,128)} %reshape.129), calls=%async_computation | async-start | bytes 131072 | tf_op jit(solution)/shard_map/all_to_all | solution.py:89
  71.9 4.0 %all-to-all-done = f32[2,1,8192]{2,1,0:T(1,128)S(1)} async-done(((f32[2,1,8192]{2,1,0:T(1,128)}), f32[2,1,8192]{2,1,0:T(1,128)S(1)}, u32[]{:S(2)}, u32[]{:S(2)}) %all-to-all-start) | async-done | bytes 65568 | tf_op jit(solution)/shard_map/all_to_all | solution.py:89
  76.5 0.8 reduce
  78.4 0.9 reshape.131
  79.3 3.9 %all-to-all-start.1 = ((f32[4,1,4096]{2,1,0:T(1,128)}), f32[4,1,4096]{2,1,0:T(1,128)S(1)}, u32[]{:S(2)}, u32[]{:S(2)}) async-start(f32[4,1,4096]{2,1,0:T(1,128)} %reshape.131), calls=%async_computation.1 | async-start | bytes 131072 | tf_op jit(solution)/shard_map/all_to_all | solution.py:91
  83.2 4.0 %all-to-all-done.1 = f32[4,1,4096]{2,1,0:T(1,128)S(1)} async-done(((f32[4,1,4096]{2,1,0:T(1,128)}), f32[4,1,4096]{2,1,0:T(1,128)S(1)}, u32[]{:S(2)}, u32[]{:S(2)}) %all-to-all-start.1) | async-done | bytes 65568 | tf_op jit(solution)/shard_map/all_to_all | solution.py:91
  87.2 0.8 reduce.1
  90.0 5.0 %all-to-all-start.2 = ((f32[8,1,2048]{2,1,0:T(1,128)}), f32[8,1,2048]{2,1,0:T(1,128)S(1)}, u32[]{:S(2)}, u32[]{:S(2)}) async-start(f32[8,1,2048]{2,1,0:T(1,128)} %reshape.133), calls=%async_computation.2 | async-start | bytes 131072 | tf_op jit(solution)/shard_map/all_to_all | solution.py:93
  94.9 1.3 fusion.102
  96.2 3.9 %collective-permute-start.6 = (f32[1,64,256]{2,0,1:T(1,128)S(1)}, f32[1,64,256]{2,0,1:T(1,128)S(1)}, u32[]{:S(2)}, u32[]{:S(2)}) collective-permute-start(f32[1,64,256]{2,0,1:T(1,128)S(1)} %get-tuple-element.28), channel_id=1, source_target_pairs={{8,0},{16,8},{24,16},{0,24},{9,1},{17,9},{25,17},{1,25},{10,2},{18... | collective-permute-start | bytes 196616 | tf_op jit(solution)/shard_map/ppermute | solution.py:24
  100.1 2.2 all-to-all-done.2
  105.3 3.8 %all-to-all-start.3 = ((f32[8,1,2048]{2,1,0:T(1,128)}), f32[8,1,2048]{2,1,0:T(1,128)S(1)}, u32[]{:S(2)}, u32[]{:S(2)}) async-start(f32[8,1,2048]{2,1,0:T(1,128)} %reshape.135), calls=%async_computation.3 | async-start | bytes 131072 | tf_op jit(solution)/shard_map/all_to_all | solution.py:109
  109.1 0.9 pad_maximum_fusion.60
  110.6 5.4 %all-to-all-done.3 = f32[8,1,2048]{2,1,0:T(1,128)S(1)} async-done(((f32[8,1,2048]{2,1,0:T(1,128)}), f32[8,1,2048]{2,1,0:T(1,128)S(1)}, u32[]{:S(2)}, u32[]{:S(2)}) %all-to-all-start.3) | async-done | bytes 65568 | tf_op jit(solution)/shard_map/all_to_all | solution.py:109
  118.5 3.3 %all-to-all-start.4 = ((f32[4,1,4096]{2,1,0:T(1,128)}), f32[4,1,4096]{2,1,0:T(1,128)S(1)}, u32[]{:S(2)}, u32[]{:S(2)}) async-start(f32[4,1,4096]{2,1,0:T(1,128)} %reshape.137), calls=%async_computation.4 | async-start | bytes 131072 | tf_op jit(solution)/shard_map/all_to_all | solution.py:111
  121.8 4.2 %pad_maximum_fusion.1 = f32[66,66,256]{2,0,1:T(8,128)} fusion(f32[66,1,256]{2,0,1:T(8,128)S(1)} %collective-permute-done.8, f32[1,64,256]{2,0,1:T(1,128)S(1)} %collective-permute-done.6, f32[64,64,256]{2,0,1:T(8,128)} %get-tuple-element.11, f32[1,64,256]{2,0,1:T(1,128)S(1)} %collective-permute-done.7, f32[66,1,256]{2,0,1:T(8,128)S(1)} %collective-permute-done.9), kind=kLoop, calls=%fused_computation.1 | loop fusion | flops 4460544 | bytes 8921088 | tf_op jit(solution)/shard_map/concatenate | solution.py:20
  126.0 0.8 reduce.4
  128.0 0.8 reshape.139
  128.8 3.5 %all-to-all-start.5 = ((f32[2,1,8192]{2,1,0:T(1,128)}), f32[2,1,8192]{2,1,0:T(1,128)S(1)}, u32[]{:S(2)}, u32[]{:S(2)}) async-start(f32[2,1,8192]{2,1,0:T(1,128)} %reshape.139), calls=%async_computation.5 | async-start | bytes 131072 | tf_op jit(solution)/shard_map/all_to_all | solution.py:113
  132.3 4.6 %fusion.99 = (f32[66,66,1]{2,0,1:T(8,128)}, f32[66,66,1]{2,0,1:T(8,128)S(1)}) fusion(f32[66,66,256]{2,0,1:T(8,128)} %pad_maximum_fusion.1), kind=kLoop, calls=%fused_computation.188 | loop fusion | bytes 69696 | tf_op jit(solution)/shard_map/slice | solution.py:18
  136.9 2.6 copy.72
  139.5 2.0 collective-permute-start.10
  141.5 0.9 copy.74
  142.5 1.0 collective-permute-done.10
  143.5 1.0 copy.73
  144.5 2.0 collective-permute-done.11
  146.5 2.4 copy.75
  148.8 0.8 reduce.5
  150.4 3.0 %broadcast_in_dim.2 = f32[16,4,16,4,256]{4,1,0,3,2:T(4,128)} broadcast(f32[16,16,256]{2,0,1:T(8,128)S(1)} %fusion.24), dimensions={0,2,4} | broadcast | bytes 4456448 | tf_op jit(solution)/shard_map/broadcast_in_dim | solution.py:115
  153.4 5.3 %reshape.118 = f32[64,64,256]{2,0,1:T(8,128)} reshape(f32[16,4,16,4,256]{4,1,0,3,2:T(4,128)} %broadcast_in_dim.2) | data formatting | bytes 8388608 | tf_op jit(solution)/shard_map/reshape | solution.py:117
  158.7 24.0 %fusion.11 = f32[64,64,256]{2,0,1:T(8,128)S(1)} fusion(f32[64,64,256]{2,0,1:T(8,128)} %reshape.118, f32[64,64,256]{2,0,1:T(8,128)} %get-tuple-element.12, f32[66,66,1]{2,0,1:T(8,128)} %copy.75, f32[66,1,256]{2,0,1:T(8,128)S(1)} %collective-permute-done.8, f32[66,1,256]{2,0,1:T(8,128)S(1)} %collective-permute-done.9, ...), kind=kLoop, calls=%fused_computation.33 | loop fusion | flops 28311552 | bytes 21272608 | tf_op jit(solution)/shard_map/add | solution.py:118
  183.5 1.5 collective-permute-start.13
  184.9 2.9 %collective-permute-done.12 = f32[1,64,256]{2,0,1:T(1,128)S(1)} collective-permute-done((f32[1,64,256]{2,0,1:T(1,128)S(1)}, f32[1,64,256]{2,0,1:T(1,128)S(1)}, u32[]{:S(2)}, u32[]{:S(2)}) %collective-permute-start.12) | collective-permute-done | bytes 65568 | tf_op jit(solution)/shard_map/ppermute | solution.py:24
  187.8 1.7 collective-permute-done.13
  190.3 1.3 collective-permute-done.14
  191.6 3.1 %collective-permute-done.15 = f32[66,1,256]{2,0,1:T(8,128)S(1)} collective-permute-done((f32[66,1,256]{2,0,1:T(8,128)S(1)}, f32[66,1,256]{2,0,1:T(8,128)S(1)}, u32[]{:S(2)}, u32[]{:S(2)}) %collective-permute-start.15) | collective-permute-done | bytes 67616 | tf_op jit(solution)/shard_map/ppermute | solution.py:22
  194.7 0.8 pad_maximum_fusion.2
  195.6 2.2 fusion.98
  197.8 2.6 copy.95
  200.7 0.9 copy.97
  201.6 1.8 collective-permute-start.17
  203.4 6.6 %copy.100 = f32[64,64,256]{2,1,0:T(8,128)} copy(f32[64,64,256]{2,0,1:T(8,128)} %copy-done) | data formatting | bytes 8388608
  210.0 1.0 copy.96
  211.0 2.4 copy.98
  213.4 24.6 %multiply_reduce_fusion = (f32[]{:T(128)}, f32[64,64,256]{2,0,1:T(8,128)S(1)}) fusion(f32[66,1,256]{2,0,1:T(8,128)S(1)} %collective-permute-done.14, f32[1,64,256]{2,0,1:T(1,128)S(1)} %collective-permute-done.12, f32[64,64,256]{2,0,1:T(8,128)} %copy-done, f32[1,64,256]{2,0,1:T(1,128)S(1)} %collective-permute-done.13, ...), kind=kLoop, calls=%fused_computation.80 | loop fusion | flops 29360128 | bytes 12884004 | tf_op jit(solution)/shard_map/reduce_sum | solution.py:121
  238.0 4.4 %copy.101 = f32[64,64,256]{2,1,0:T(8,128)} copy(f32[64,64,256]{2,0,1:T(8,128)S(1)} %get-tuple-element.10) | data formatting | bytes 8388608
  242.5 37.5 %psum.7 = f32[]{:T(128)} all-reduce(f32[]{:T(128)} %get-tuple-element.9), channel_id=1, replica_groups=mesh['gx'=4,'gy'=4,'gz'=2] {'gx','gy','gz'}, use_global_device_ids=true, to_apply=%region_2.3 | all-reduce | flops 1 | bytes 8 | tf_op jit(solution)/shard_map/psum | solution.py:121
  (75 shorter events, 17.0 us)
Async XLA Ops:
  1.6 11.9 %collective-permute-start = (f32[1,64,256]{2,0,1:T(1,128)S(1)}, f32[1,64,256]{2,0,1:T(1,128)S(1)}, u32[]{:S(2)}, u32[]{:S(2)}) collective-permute-start(f32[1,64,256]{2,0,1:T(1,128)S(1)} %copy.62), channel_id=1, source_target_pairs={{8,0},{16,8},{24,16},{0,24},{9,1},{17,9},{25,17},{1,25},{10,2},{18... | collective-permute-start | bytes 196616 | tf_op jit(solution)/shard_map/ppermute | solution.py:24
  6.8 6.7 %collective-permute-start.1 = (f32[1,64,256]{2,0,1:T(1,128)S(1)}, f32[1,64,256]{2,0,1:T(1,128)S(1)}, u32[]{:S(2)}, u32[]{:S(2)}) collective-permute-start(f32[1,64,256]{2,0,1:T(1,128)S(1)} %copy.64), channel_id=1, source_target_pairs={{0,8},{8,16},{16,24},{24,0},{1,9},{9,17},{17,25},{25,1},{2,10},{10... | collective-permute-start | bytes 196616 | tf_op jit(solution)/shard_map/ppermute | solution.py:22
  13.5 5.9 %copy-start.1 = (f32[64,64,256]{2,0,1:T(8,128)S(1)}, f32[64,64,256]{2,0,1:T(8,128)}, u32[]{:S(2)}) copy-start(f32[64,64,256]{2,0,1:T(8,128)} %copy.76) | copy-start | bytes 12582916
  14.6 2.7 collective-permute-start.2
  15.3 4.1 %collective-permute-start.3 = (f32[66,1,256]{2,0,1:T(8,128)S(1)}, f32[66,1,256]{2,0,1:T(8,128)S(1)}, u32[]{:S(2)}, u32[]{:S(2)}) collective-permute-start(f32[66,1,256]{2,0,1:T(8,128)S(1)} %get-tuple-element.23), channel_id=1, source_target_pairs={{0,2},{2,4},{4,6},{6,0},{1,3},{3,5},{5,7},{7,1},{8,10},{10,12},{12... | collective-permute-start | bytes 202760 | tf_op jit(solution)/shard_map/ppermute | solution.py:22
  24.9 4.3 %collective-permute-start.4 = (f32[66,66,1]{1,0,2:T(8,128)S(1)}, f32[66,66,1]{1,0,2:T(8,128)S(1)}, u32[]{:S(2)}, u32[]{:S(2)}) collective-permute-start(f32[66,66,1]{1,0,2:T(8,128)S(1)} %copy.67), channel_id=1, source_target_pairs={{1,0},{0,1},{3,2},{2,3},{5,4},{4,5},{7,6},{6,7},{9,8},{8,9},{11,10... | collective-permute-start | bytes 52280 | tf_op jit(solution)/shard_map/ppermute | solution.py:24
  27.4 4.0 %collective-permute-start.5 = (f32[66,66,1]{1,0,2:T(8,128)S(1)}, f32[66,66,1]{1,0,2:T(8,128)S(1)}, u32[]{:S(2)}, u32[]{:S(2)}) collective-permute-start(f32[66,66,1]{1,0,2:T(8,128)S(1)} %copy.69), channel_id=1, source_target_pairs={{0,1},{1,0},{2,3},{3,2},{4,5},{5,4},{6,7},{7,6},{8,9},{9,8},{10,11... | collective-permute-start | bytes 52280 | tf_op jit(solution)/shard_map/ppermute | solution.py:22
  68.5 7.4 %all-to-all-start = ((f32[2,1,8192]{2,1,0:T(1,128)}), f32[2,1,8192]{2,1,0:T(1,128)S(1)}, u32[]{:S(2)}, u32[]{:S(2)}) async-start(f32[2,1,8192]{2,1,0:T(1,128)} %reshape.129), calls=%async_computation | async-start | bytes 131072 | tf_op jit(solution)/shard_map/all_to_all | solution.py:89
  79.3 8.0 %all-to-all-start.1 = ((f32[4,1,4096]{2,1,0:T(1,128)}), f32[4,1,4096]{2,1,0:T(1,128)S(1)}, u32[]{:S(2)}, u32[]{:S(2)}) async-start(f32[4,1,4096]{2,1,0:T(1,128)} %reshape.131), calls=%async_computation.1 | async-start | bytes 131072 | tf_op jit(solution)/shard_map/all_to_all | solution.py:91
  90.0 12.3 %all-to-all-start.2 = ((f32[8,1,2048]{2,1,0:T(1,128)}), f32[8,1,2048]{2,1,0:T(1,128)S(1)}, u32[]{:S(2)}, u32[]{:S(2)}) async-start(f32[8,1,2048]{2,1,0:T(1,128)} %reshape.133), calls=%async_computation.2 | async-start | bytes 131072 | tf_op jit(solution)/shard_map/all_to_all | solution.py:93
  96.2 12.9 %collective-permute-start.6 = (f32[1,64,256]{2,0,1:T(1,128)S(1)}, f32[1,64,256]{2,0,1:T(1,128)S(1)}, u32[]{:S(2)}, u32[]{:S(2)}) collective-permute-start(f32[1,64,256]{2,0,1:T(1,128)S(1)} %get-tuple-element.28), channel_id=1, source_target_pairs={{8,0},{16,8},{24,16},{0,24},{9,1},{17,9},{25,17},{1,25},{10,2},{18... | collective-permute-start | bytes 196616 | tf_op jit(solution)/shard_map/ppermute | solution.py:24
  100.1 9.0 %collective-permute-start.7 = (f32[1,64,256]{2,0,1:T(1,128)S(1)}, f32[1,64,256]{2,0,1:T(1,128)S(1)}, u32[]{:S(2)}, u32[]{:S(2)}) collective-permute-start(f32[1,64,256]{2,0,1:T(1,128)S(1)} %get-tuple-element.27), channel_id=1, source_target_pairs={{0,8},{8,16},{16,24},{24,0},{1,9},{9,17},{17,25},{25,1},{2,10},{10... | collective-permute-start | bytes 196616 | tf_op jit(solution)/shard_map/ppermute | solution.py:22
  105.3 10.7 %all-to-all-start.3 = ((f32[8,1,2048]{2,1,0:T(1,128)}), f32[8,1,2048]{2,1,0:T(1,128)S(1)}, u32[]{:S(2)}, u32[]{:S(2)}) async-start(f32[8,1,2048]{2,1,0:T(1,128)} %reshape.135), calls=%async_computation.3 | async-start | bytes 131072 | tf_op jit(solution)/shard_map/all_to_all | solution.py:109
  110.0 11.7 %collective-permute-start.8 = (f32[66,1,256]{2,0,1:T(8,128)S(1)}, f32[66,1,256]{2,0,1:T(8,128)S(1)}, u32[]{:S(2)}, u32[]{:S(2)}) collective-permute-start(f32[66,1,256]{2,0,1:T(8,128)S(1)} %get-tuple-element.22), channel_id=1, source_target_pairs={{2,0},{4,2},{6,4},{0,6},{3,1},{5,3},{7,5},{1,7},{10,8},{12,10},{14... | collective-permute-start | bytes 202760 | tf_op jit(solution)/shard_map/ppermute | solution.py:24
  110.1 11.7 %collective-permute-start.9 = (f32[66,1,256]{2,0,1:T(8,128)S(1)}, f32[66,1,256]{2,0,1:T(8,128)S(1)}, u32[]{:S(2)}, u32[]{:S(2)}) collective-permute-start(f32[66,1,256]{2,0,1:T(8,128)S(1)} %get-tuple-element.21), channel_id=1, source_target_pairs={{0,2},{2,4},{4,6},{6,0},{1,3},{3,5},{5,7},{7,1},{8,10},{10,12},{12... | collective-permute-start | bytes 202760 | tf_op jit(solution)/shard_map/ppermute | solution.py:22
  118.5 7.5 %all-to-all-start.4 = ((f32[4,1,4096]{2,1,0:T(1,128)}), f32[4,1,4096]{2,1,0:T(1,128)S(1)}, u32[]{:S(2)}, u32[]{:S(2)}) async-start(f32[4,1,4096]{2,1,0:T(1,128)} %reshape.137), calls=%async_computation.4 | async-start | bytes 131072 | tf_op jit(solution)/shard_map/all_to_all | solution.py:111
  128.8 20.0 %all-to-all-start.5 = ((f32[2,1,8192]{2,1,0:T(1,128)}), f32[2,1,8192]{2,1,0:T(1,128)S(1)}, u32[]{:S(2)}, u32[]{:S(2)}) async-start(f32[2,1,8192]{2,1,0:T(1,128)} %reshape.139), calls=%async_computation.5 | async-start | bytes 131072 | tf_op jit(solution)/shard_map/all_to_all | solution.py:113
  139.5 4.0 %collective-permute-start.10 = (f32[66,66,1]{1,0,2:T(8,128)S(1)}, f32[66,66,1]{1,0,2:T(8,128)S(1)}, u32[]{:S(2)}, u32[]{:S(2)}) collective-permute-start(f32[66,66,1]{1,0,2:T(8,128)S(1)} %copy.72), channel_id=1, source_target_pairs={{1,0},{0,1},{3,2},{2,3},{5,4},{4,5},{7,6},{6,7},{9,8},{8,9},{11,10... | collective-permute-start | bytes 52280 | tf_op jit(solution)/shard_map/ppermute | solution.py:24
  142.5 4.0 %collective-permute-start.11 = (f32[66,66,1]{1,0,2:T(8,128)S(1)}, f32[66,66,1]{1,0,2:T(8,128)S(1)}, u32[]{:S(2)}, u32[]{:S(2)}) collective-permute-start(f32[66,66,1]{1,0,2:T(8,128)S(1)} %copy.74), channel_id=1, source_target_pairs={{0,1},{1,0},{2,3},{3,2},{4,5},{5,4},{6,7},{7,6},{8,9},{9,8},{10,11... | collective-permute-start | bytes 52280 | tf_op jit(solution)/shard_map/ppermute | solution.py:22
  182.8 12.8 %copy-start = (f32[64,64,256]{2,0,1:T(8,128)}, f32[64,64,256]{2,0,1:T(8,128)S(1)}, u32[]{:S(2)}) copy-start(f32[64,64,256]{2,0,1:T(8,128)S(1)} %fusion.11) | copy-start | bytes 12582916
  182.9 5.0 %collective-permute-start.12 = (f32[1,64,256]{2,0,1:T(1,128)S(1)}, f32[1,64,256]{2,0,1:T(1,128)S(1)}, u32[]{:S(2)}, u32[]{:S(2)}) collective-permute-start(f32[1,64,256]{2,0,1:T(1,128)S(1)} %get-tuple-element.26), channel_id=1, source_target_pairs={{8,0},{16,8},{24,16},{0,24},{9,1},{17,9},{25,17},{1,25},{10,2},{18... | collective-permute-start | bytes 196616 | tf_op jit(solution)/shard_map/ppermute | solution.py:24
  183.5 6.1 %collective-permute-start.13 = (f32[1,64,256]{2,0,1:T(1,128)S(1)}, f32[1,64,256]{2,0,1:T(1,128)S(1)}, u32[]{:S(2)}, u32[]{:S(2)}) collective-permute-start(f32[1,64,256]{2,0,1:T(1,128)S(1)} %get-tuple-element.25), channel_id=1, source_target_pairs={{0,8},{8,16},{16,24},{24,0},{1,9},{9,17},{17,25},{25,1},{2,10},{10... | collective-permute-start | bytes 196616 | tf_op jit(solution)/shard_map/ppermute | solution.py:22
  189.6 2.0 collective-permute-start.14
  189.6 5.1 %collective-permute-start.15 = (f32[66,1,256]{2,0,1:T(8,128)S(1)}, f32[66,1,256]{2,0,1:T(8,128)S(1)}, u32[]{:S(2)}, u32[]{:S(2)}) collective-permute-start(f32[66,1,256]{2,0,1:T(8,128)S(1)} %get-tuple-element.19), channel_id=1, source_target_pairs={{0,2},{2,4},{4,6},{6,0},{1,3},{3,5},{5,7},{7,1},{8,10},{10,12},{12... | collective-permute-start | bytes 202760 | tf_op jit(solution)/shard_map/ppermute | solution.py:22
  200.4 9.7 %collective-permute-start.16 = (f32[66,66,1]{1,0,2:T(8,128)S(1)}, f32[66,66,1]{1,0,2:T(8,128)S(1)}, u32[]{:S(2)}, u32[]{:S(2)}) collective-permute-start(f32[66,66,1]{1,0,2:T(8,128)S(1)} %copy.95), channel_id=1, source_target_pairs={{1,0},{0,1},{3,2},{2,3},{5,4},{4,5},{7,6},{6,7},{9,8},{8,9},{11,10... | collective-permute-start | bytes 52280 | tf_op jit(solution)/shard_map/ppermute | solution.py:24
  201.6 9.4 %collective-permute-start.17 = (f32[66,66,1]{1,0,2:T(8,128)S(1)}, f32[66,66,1]{1,0,2:T(8,128)S(1)}, u32[]{:S(2)}, u32[]{:S(2)}) collective-permute-start(f32[66,66,1]{1,0,2:T(8,128)S(1)} %copy.97), channel_id=1, source_target_pairs={{0,1},{1,0},{2,3},{3,2},{4,5},{5,4},{6,7},{7,6},{8,9},{9,8},{10,11... | collective-permute-start | bytes 52280 | tf_op jit(solution)/shard_map/ppermute | solution.py:22
where the time goes:
time: 286 us; the launch traced here: 282 us
  other arithmetic  90.1 us (32%)
  local copies, waits for them, and re-layouts  71.9 us (25%)
  starting transfers between devices  42.5 us (15%)
  blocking collectives  37.5 us (13%)
  waiting for transfers between devices  33.7 us (12%)
  matrix products  3.24 us (1%)
  between operations  3.13 us (1%)
    psum x1, blocking collectives, per_device(): total = lax.psum(jnp.sum(new_residual * new_residual), ('gx', 'gy', 'gz'))  37.5 us
    div x1, other arithmetic, per_device(): first_sweep = residual_now / diag_value  24.9 us
    reduce_sum x1, other arithmetic, per_device(): total = lax.psum(jnp.sum(new_residual * new_residual), ('gx', 'gy', 'gz'))  24.6 us
    add x1, other arithmetic, per_device(): updated = guess + local_fix + prolonged  24 us
    unnamed x19, local copies, waits for them, and re-layouts  23.5 us
    slice x7, local copies, waits for them, and re-layouts, padded_2(): head = lax.slice_in_dim(cells, 0, width, axis=dim)  16.9 us
    ppermute x9, starting transfers between devices, padded_2(): lax.ppermute(head, axis, [((i + 1) % count, i) for i in range(count)])  14.4 us
    ppermute x9, waiting for transfers between devices, padded_2(): lax.ppermute(tail, axis, [(i, (i + 1) % count) for i in range(count)])  10.1 us
  transfers between devices with their start and end apart: 24, of which 14 were waited for; matrix products, arithmetic and copies ran while one was open for 14% of the time, Pallas kernels for 0%

commit v1 on v0

v1 whole, which is shorter than its diff:
```python
import functools

import jax
import jax.numpy as jnp
import numpy as np
from jax import lax
from jax.experimental import pallas as pl
from jax.experimental.pallas import tpu as pltpu
from jax.sharding import PartitionSpec as P

COARSEN = 4
SCREEN = 0.002
DIAG = 6.0 + SCREEN
LANES = 128
EXACT = lax.Precision.HIGHEST
MESH = pl.DeviceIdType.MESH


def cas(length):
    index = np.arange(length)
    angle = 2.0 * np.pi * (np.outer(index, index) % length) / length
    return np.cos(angle) + np.sin(angle)


def eigen_line(length):
    index = np.arange(length)
    return (2.0 - 2.0 * np.cos(2.0 * np.pi * index / length)) / (COARSEN * COARSEN)


class Plan:
    def __init__(self, counts, block):
        self.px, self.py, self.pz = counts
        self.bx, self.by, self.bz = block
        self.ndev = self.px * self.py * self.pz
        self.group = self.py * self.pz
        self.cx, self.cy, self.cz = (n // COARSEN for n in block)
        self.lx, self.ly, self.lz = self.cx * self.px, self.cy * self.py, self.cz * self.pz
        self.rx = self.cx // self.group
        self.rk = self.ly // self.ndev
        assert self.rx * self.group == self.cx and self.rk * self.ndev == self.ly
        self.rows = self.rx * self.rk
        self.hr = -(-(self.cy + 2) // 8) * 8

    def tables(self):
        px, py, pz, group, ndev = self.px, self.py, self.pz, self.group, self.ndev
        cx, cy, cz, rx, rk = self.cx, self.cy, self.cz, self.rx, self.rk
        lx, ly, lz, hr = self.lx, self.ly, self.lz, self.hr
        tx, ty, tz = cas(lx), cas(ly), cas(lz)
        up_z = np.arange(self.bz) // COARSEN
        mz = np.stack([tz[g * cz + up_z] for g in range(pz)]) / COARSEN**3
        pool = (np.arange(self.by)[None, :] // COARSEN == np.arange(cy)[:, None]) * 1.0
        my = np.zeros((ndev, rx, rk, py, pz, rx, cy))
        for j in range(rx):
            part = ty.reshape(py, cy, ndev, rk).transpose(2, 3, 0, 1)
            my[:, j, :, :, :, j, :] = part[:, :, :, None, :]
        my = my.reshape(ndev * rx * rk, group * rx * cy)
        mx = np.zeros((rk, lx, px, group, rx, rk))
        for k in range(rk):
            mx[k, :, :, :, :, k] = tx.reshape(px, group, rx, lx).transpose(3, 0, 1, 2)
        mx = mx.reshape(rk * lx, ndev * rx * rk)
        mxi = mx.T / (lx * ly * lz)
        rows_of = np.arange(py)[:, None] * cy + np.concatenate([np.arange(cy), [-1, cy]])[None, :]
        lines = np.zeros((py, hr, ly))
        lines[:, : cy + 2] = ty[rows_of % ly]
        myi = np.zeros((py, rx, hr, ndev, rx, rk))
        for j in range(rx):
            myi[:, j, :, :, j, :] = lines.reshape(py, hr, ndev, rk)
        myi = myi.reshape(py * rx * hr, ndev * rx * rk)
        mzi = np.zeros((pz, lz, self.bz + LANES))
        for g in range(pz):
            mzi[g, :, : self.bz] = tz[:, g * cz + up_z]
            mzi[g, :, self.bz] = tz[:, (g * cz - 1) % lz]
            mzi[g, :, self.bz + LANES - 1] = tz[:, (g * cz + cz) % lz]
        spread = (np.arange(self.by)[:, None] // COARSEN == np.arange(hr)[None, :]) * 1.0
        ei = SCREEN + eigen_line(lx)[:, None] + eigen_line(lz)[None, :]
        ey = np.repeat(eigen_line(ly)[:, None, None], lz, axis=2)
        return [t.astype(np.float32) for t in (mz, pool, my, mx, mxi, myi, mzi, spread, ei, ey)]


def dot(a, b):
    return jnp.dot(a, b, precision=EXACT, preferred_element_type=jnp.float32)


def kernel(plan, rs_hbm, g_hbm, *refs):
    q = plan
    table_hbm = refs[:10]
    up_hbm, res_hbm, norm_out = refs[10:13]
    tabs = refs[13:23]
    mz, pool, my, mx, mxi, myi, mzi, spread, ei, ey = tabs
    (rs, g, r, u, n, yp, zp, yh, zh, pooled, first, r1, s2, r2, flat, s3, r3, s4, r4, zf, wz, nrm,
     in_sem, tab_sem, out_sem, face_send, face_recv, a_send, a_recv) = refs[23:]
    ndev, group = q.ndev, q.group
    bx, by, bz = q.bx, q.by, q.bz
    ix, iy, iz = lax.axis_index("gx"), lax.axis_index("gy"), lax.axis_index("gz")
    me_p = iy * q.pz + iz
    me = ix * group + me_p

    def coords(lin):
        return (lin // group, (lin % group) // q.pz, lin % q.pz)

    in_chunks = 4
    step = bx // in_chunks
    copies_g = [
        pltpu.make_async_copy(g_hbm.at[pl.ds(c * step, step)], g.at[pl.ds(1 + c * step, step)], in_sem.at[c])
        for c in range(in_chunks)
    ]
    copies_r = [
        pltpu.make_async_copy(rs_hbm.at[pl.ds(c * step, step)], rs.at[pl.ds(c * step, step)], in_sem.at[in_chunks + c])
        for c in range(in_chunks)
    ]
    copies_t = [pltpu.make_async_copy(a, b, tab_sem.at[i]) for i, (a, b) in enumerate(zip(table_hbm, tabs))]
    for c in copies_g + copies_r + copies_t:
        c.start()

    barrier = pltpu.get_barrier_semaphore()

    def greet(k, carry):
        pl.semaphore_signal(barrier, inc=1, device_id=coords((me + k) % ndev), device_id_type=MESH)
        return carry

    lax.fori_loop(1, ndev, greet, 0)

    lane = lax.broadcasted_iota(jnp.int32, (by, LANES), 1)
    row = lax.broadcasted_iota(jnp.int32, (by, LANES), 0)

    def pack_plane(x, v, phase, acc):
        lo, hi = acc
        yp[phase, 0, x] = v[0:1, :]
        yp[phase, 1, x] = v[by - 1 : by, :]
        lo = jnp.where(lane == x, pltpu.roll(v[:, :LANES], x, 1), lo)
        hi = jnp.where(lane == x, pltpu.roll(v[:, bz - LANES :], (x + 1) % LANES, 1), hi)
        return lo, hi

    zero_acc = (jnp.zeros((by, LANES), jnp.float32), jnp.zeros((by, LANES), jnp.float32))

    def face_copies(phase, buf):
        xl, xr = (ix + q.px - 1) % q.px, (ix + 1) % q.px
        yl, yr = (iy + q.py - 1) % q.py, (iy + 1) % q.py
        zl, zr = (iz + q.pz - 1) % q.pz, (iz + 1) % q.pz
        moves = [
            (buf.at[1], buf.at[bx + 1], (xl, iy, iz)),
            (buf.at[bx], buf.at[0], (xr, iy, iz)),
            (yp.at[phase, 0], yh.at[phase, 1], (ix, yl, iz)),
            (yp.at[phase, 1], yh.at[phase, 0], (ix, yr, iz)),
            (zp.at[phase, 0], zh.at[phase, 1], (ix, iy, zl)),
            (zp.at[phase, 1], zh.at[phase, 0], (ix, iy, zr)),
        ]
        return [
            pltpu.make_async_remote_copy(
                src_ref=s, dst_ref=d, send_sem=face_send.at[phase, i], recv_sem=face_recv.at[phase, i],
                device_id=dev, device_id_type=MESH,
            )
            for i, (s, d, dev) in enumerate(moves)
        ]

    def plane_sum(x, buf, phase, ylo, yhi, zadd):
        v = buf[x + 1]
        zlo = pltpu.roll(zh[phase, 0], (LANES - x) % LANES, 1)
        zhi = pltpu.roll(zh[phase, 1], LANES - 1 - x, 1)
        if zadd is not None:
            zlo, zhi = zlo + zadd, zhi + zadd
        tiles = [v[:, t * LANES : (t + 1) * LANES] for t in range(bz // LANES)]
        up = [pltpu.roll(t, 1, 1) for t in tiles]
        down = [pltpu.roll(t, LANES - 1, 1) for t in tiles]
        out = []
        for t, c in enumerate(tiles):
            cols = slice(t * LANES, (t + 1) * LANES)
            total = buf[x, :, cols] + buf[x + 2, :, cols]
            total += jnp.where(row == 0, ylo[:, cols], pltpu.roll(c, 1, 0))
            total += jnp.where(row == by - 1, yhi[:, cols], pltpu.roll(c, by - 1, 0))
            total += jnp.where(lane == 0, up[t - 1] if t > 0 else zlo, up[t])
            total += jnp.where(lane == LANES - 1, down[t + 1] if t + 1 < len(tiles) else zhi, down[t])
            out.append(total)
        return v, jnp.concatenate(out, axis=1)

    for c in copies_g:
        c.wait()
    lo, hi = lax.fori_loop(0, bx, lambda x, acc: pack_plane(x, g[x + 1], 0, acc), zero_acc, unroll=4)
    zp[0, 0], zp[0, 1] = lo, hi
    pl.semaphore_wait(barrier, ndev - 1)
    faces0 = face_copies(0, g)
    for c in faces0:
        c.start()
    for c in copies_r:
        c.wait()
    for c in faces0:
        c.wait_recv()

    def residual_four(i, acc):
        total = jnp.zeros((by, bz), jnp.float32)
        for a in range(COARSEN):
            x = i * COARSEN + a
            v, around = plane_sum(x, g, 0, yh[0, 0, x], yh[0, 1, x], None)
            res = rs[x] - (DIAG * v - around)
            r[x + 1] = res
            total += res
            acc = pack_plane(x, res, 1, acc)
        pooled[i] = total
        return acc

    lo, hi = lax.fori_loop(0, q.cx, residual_four, zero_acc)
    zp[1, 0], zp[1, 1] = lo, hi
    for c in copies_t:
        c.wait()

    def fold_rows(i, carry):
        zf[i, : q.cy, :bz] = dot(pool[...], pooled[i])
        return carry

    lax.fori_loop(0, q.cx, fold_rows, 0, unroll=True)
    cells = zf[: q.cx, : q.cy, :bz].reshape(q.cx * q.cy, bz)
    first[...] = dot(cells, mz[iz]).reshape(first.shape)

    def spread_out(src, dst, stage, peers, here, device_of, own):
        def send(k, carry):
            d = (here + k) % peers
            pltpu.make_async_remote_copy(
                src_ref=src.at[d], dst_ref=dst.at[here], send_sem=a_send.at[stage], recv_sem=a_recv.at[stage],
                device_id=device_of(d), device_id_type=MESH,
            ).start()
            return carry

        lax.fori_loop(1, peers, send, 0)
        dst[here] = own

    def all_bytes(dst, count, sem):
        part = dst.at[pl.ds(0, count)]
        pltpu.make_async_copy(part, part, sem).wait()

    in_group = lambda d: (ix, d // q.pz, d % q.pz)
    spread_out(first, r1, 0, group, me_p, in_group, first[me_p])
    faces1 = face_copies(1, r)
    for c in faces1:
        c.start()

    def fix_planes(start, stop, acc):
        def body(x, acc):
            v, around = plane_sum(x, r, 1, yh[1, 0, x], yh[1, 1, x], None)
            out = g[x + 1] + (v + around * (1.0 / DIAG)) * (1.0 / DIAG)
            u[x + 1] = out
            return pack_plane(x, out, 2, acc)

        return lax.fori_loop(start, stop, body, acc, unroll=2)

    all_bytes(r1, group - 1, a_recv.at[0])
    lines = dot(my[...], r1[...].reshape(group * q.rx * q.cy, q.lz))
    for d in range(ndev):
        s2[d] = lines[d * q.rows : (d + 1) * q.rows]
    spread_out(s2, r2, 1, ndev, me, coords, s2[me])
    for c in faces1:
        c.wait_recv()
    acc = fix_planes(0, bx // 2, zero_acc)
    all_bytes(r2, ndev - 1, a_recv.at[1])
    for d in range(ndev):
        flat[d * q.rows : (d + 1) * q.rows] = r2[d]
    spec = dot(mx[...], flat[...])
    spec = jnp.concatenate(
        [spec[k * q.lx : (k + 1) * q.lx] / (ei[...] + ey[me * q.rk + k]) for k in range(q.rk)], axis=0
    )
    lines = dot(mxi[...], spec)
    for d in range(ndev):
        s3[d] = lines[d * q.rows : (d + 1) * q.rows]
    spread_out(s3, r3, 2, ndev, me, coords, s3[me])
    lo, hi = fix_planes(bx // 2, bx, acc)
    zp[2, 0], zp[2, 1] = lo, hi
    faces2 = face_copies(2, u)
    for c in faces2:
        c.start()
    all_bytes(r3, ndev - 1, a_recv.at[2])
    for d in range(ndev):
        flat[d * q.rows : (d + 1) * q.rows] = r3[d]
    s4[...] = dot(myi[...], flat[...]).reshape(s4.shape)

    def send_lines(k, carry):
        d = (me_p + k) % group
        pltpu.make_async_remote_copy(
            src_ref=s4.at[d // q.pz], dst_ref=r4.at[pl.ds(me_p * q.rx, q.rx)],
            send_sem=a_send.at[3], recv_sem=a_recv.at[3], device_id=in_group(d), device_id_type=MESH,
        ).start()
        return carry

    lax.fori_loop(1, group, send_lines, 0)
    r4[pl.ds(me_p * q.rx, q.rx)] = s4[iy]

    def edge(to_x, j, slot, sem):
        def send(d, carry):
            pltpu.make_async_remote_copy(
                src_ref=s4.at[d // q.pz, j], dst_ref=r4.at[slot], send_sem=a_send.at[sem], recv_sem=a_recv.at[sem],
                device_id=(to_x, d // q.pz, d % q.pz), device_id_type=MESH,
            ).start()
            return carry

        lax.fori_loop(0, group, send, 0)

    @pl.when(me_p == group - 1)
    def _():
        edge((ix + 1) % q.px, q.rx - 1, q.cx, 4)

    @pl.when(me_p == 0)
    def _():
        edge((ix + q.px - 1) % q.px, 0, q.cx + 1, 5)

    all_bytes(r4, (group - 1) * q.rx, a_recv.at[3])
    all_bytes(r4, 1, a_recv.at[4])
    all_bytes(r4, 1, a_recv.at[5])
    zf[...] = dot(r4[...].reshape((q.cx + 2) * q.hr, q.lz), mzi[iz]).reshape(zf.shape)

    def prolong(i, carry):
        fine = dot(spread[...], zf[i])
        wz[i] = fine[:, bz:]
        for a in range(COARSEN):
            u[1 + i * COARSEN + a] += fine[:, :bz]
        return carry

    for c in faces2:
        c.wait_send()
    lax.fori_loop(0, q.cx, prolong, 0)
    out_u = pltpu.make_async_copy(u.at[pl.ds(1, bx)], up_hbm, out_sem.at[0])
    out_u.start()
    for c in faces2:
        c.wait_recv()
    u[0] += dot(spread[...], zf[q.cx])[:, :bz]
    u[bx + 1] += dot(spread[...], zf[q.cx + 1])[:, :bz]

    out_planes = bx // in_chunks
    outs_n = []
    total = jnp.zeros((by, bz), jnp.float32)
    for c in range(in_chunks):

        def last_four(i, total):
            ylo, yhi = zf[i, q.cy : q.cy + 1, :bz], zf[i, q.cy + 1 : q.cy + 2, :bz]
            for a in range(COARSEN):
                x = i * COARSEN + a
                v, around = plane_sum(x, u, 2, yh[2, 0, x] + ylo, yh[2, 1, x] + yhi, wz[i])
                res = rs[x] - (DIAG * v - around)
                n[x] = res
                total += res * res
            return total

        total = lax.fori_loop(c * q.cx // in_chunks, (c + 1) * q.cx // in_chunks, last_four, total)
        cp = pltpu.make_async_copy(
            n.at[pl.ds(c * out_planes, out_planes)], res_hbm.at[pl.ds(c * out_planes, out_planes)], out_sem.at[1 + c]
        )
        cp.start()
        outs_n.append(cp)

    line = jnp.sum(total, axis=0, keepdims=True)
    part = line[:, :LANES]
    for t in range(1, bz // LANES):
        part = part + line[:, t * LANES : (t + 1) * LANES]
    nrm[me] = part

    def send_norm(k, carry):
        d = (me + k) % ndev
        pltpu.make_async_remote_copy(
            src_ref=nrm.at[me], dst_ref=nrm.at[me], send_sem=a_send.at[6], recv_sem=a_recv.at[6],
            device_id=coords(d), device_id_type=MESH,
        ).start()
        return carry

    lax.fori_loop(1, ndev, send_norm, 0)
    all_bytes(nrm, ndev - 1, a_recv.at[6])
    norm_out[...] = jnp.sqrt(jnp.sum(jnp.sum(nrm[...], axis=0), axis=1, keepdims=True)).reshape(1, 1)

    all_bytes(nrm, ndev - 1, a_send.at[6])
    all_bytes(first, group - 1, a_send.at[0])
    all_bytes(s2, ndev - 1, a_send.at[1])
    all_bytes(s3, ndev - 1, a_send.at[2])
    all_bytes(r4, (group - 1) * q.rx, a_send.at[3])

    @pl.when(me_p == group - 1)
    def _():
        all_bytes(r4, group, a_send.at[4])

    @pl.when(me_p == 0)
    def _():
        all_bytes(r4, group, a_send.at[5])

    for c in faces0 + faces1:
        c.wait_send()
    out_u.wait()
    for cp in outs_n:
        cp.wait()


def per_device(right_side, guess):
    counts = tuple(lax.axis_size(a) for a in ("gx", "gy", "gz"))
    q = Plan(counts, guess.shape)
    assert q.lz == LANES and q.bx <= LANES and q.bz % LANES == 0
    tables = q.tables()
    f32 = jnp.float32
    bx, by, bz = guess.shape
    vm = lambda *shape: pltpu.VMEM(shape, f32)
    scratch = [vm(*t.shape) for t in tables] + [
        vm(bx, by, bz), vm(bx + 2, by, bz), vm(bx + 2, by, bz), vm(bx + 2, by, bz), vm(bx, by, bz),
        vm(3, 2, bx, 1, bz), vm(3, 2, by, LANES), vm(3, 2, bx, 1, bz), vm(3, 2, by, LANES),
        vm(q.cx, by, bz),
        vm(q.group, q.rx, q.cy, q.lz), vm(q.group, q.rx, q.cy, q.lz),
        vm(q.ndev, q.rows, q.lz), vm(q.ndev, q.rows, q.lz), vm(q.ndev * q.rows, q.lz),
        vm(q.ndev, q.rows, q.lz), vm(q.ndev, q.rows, q.lz),
        vm(q.py, q.rx, q.hr, q.lz), vm(q.cx + 2, q.hr, q.lz),
        vm(q.cx + 2, q.hr, bz + LANES), vm(q.cx, by, LANES), vm(q.ndev, 1, LANES),
        pltpu.SemaphoreType.DMA((8,)), pltpu.SemaphoreType.DMA((len(tables),)), pltpu.SemaphoreType.DMA((5,)),
        pltpu.SemaphoreType.DMA((3, 6)), pltpu.SemaphoreType.DMA((3, 6)),
        pltpu.SemaphoreType.DMA((7,)), pltpu.SemaphoreType.DMA((7,)),
    ]
    updated, new_residual, norm = pl.pallas_call(
        functools.partial(kernel, q),
        out_shape=[
            jax.ShapeDtypeStruct(guess.shape, f32),
            jax.ShapeDtypeStruct(guess.shape, f32),
            jax.ShapeDtypeStruct((1, 1), f32),
        ],
        in_specs=[pl.BlockSpec(memory_space=pl.ANY)] * (2 + len(tables)),
        out_specs=[
            pl.BlockSpec(memory_space=pl.ANY),
            pl.BlockSpec(memory_space=pl.ANY),
            pl.BlockSpec(memory_space=pltpu.VMEM),
        ],
        scratch_shapes=scratch,
        compiler_params=pltpu.CompilerParams(
            collective_id=0, has_side_effects=True, vmem_limit_bytes=60 * 1024 * 1024
        ),
        name="schwarz_step",
    )(right_side, guess, *[jnp.asarray(t) for t in tables])
    return updated, new_residual, norm[0, 0]


def solution(mesh):
    return jax.shard_map(
        per_device,
        mesh=mesh,
        in_specs=(P("gx", "gy", "gz"), P("gx", "gy", "gz")),
        out_specs=(P("gx", "gy", "gz"), P("gx", "gy", "gz"), P()),
        check_vma=False,
    )
```

time: 286 us -> 73.4 us (0.26); the launches traced: 282 us -> 73.2 us
  other arithmetic: 90.1 us -> 0 us
  local copies, waits for them, and re-layouts: 71.9 us -> 6.87 us
  Pallas kernels: 0 us -> 64 us
  starting transfers between devices: 42.5 us -> 0 us
  blocking collectives: 37.5 us -> 0 us
  waiting for transfers between devices: 33.7 us -> 0 us
  matrix products: 3.24 us -> 0 us
    pallas_call x0 -> x1, Pallas kernels: none -> 64 us  [per_device(): pl.pallas_call(functools.partial(kernel, q), out_shape=[jax.ShapeDtypeStr...]
    psum x1 -> x0, blocking collectives: 37.5 us -> none  [per_device(): total = lax.psum(jnp.sum(new_residual * new_residual), ('gx', 'gy', 'gz'))]
    reduce_sum x2 -> x0, other arithmetic: 28.2 us -> none  [the longest x1 24.6 us: per_device(): total = lax.psum(jnp.sum(new_residual * new_residual), ('gx', 'gy', 'gz'))]
    div x4 -> x0, other arithmetic: 25.1 us -> none  [the longest x1 24.9 us: per_device(): first_sweep = residual_now / diag_value]
    add x3 -> x0, other arithmetic: 24.2 us -> none  [the longest x1 24 us: per_device(): updated = guess + local_fix + prolonged]
    all_to_all x6 -> x0, starting transfers between devices: 22.7 us -> none  [the longest x1 4.96 us: per_device(): lax.all_to_all(spectra, ('gx', 'gz'), split_axis=1, concat_axis=0, tiled=...]
    slice x14 -> x0, local copies, waits for them, and re-layouts: 21.9 us -> none  [the longest x7 16.9 us: padded_2(): head = lax.slice_in_dim(cells, 0, width, axis=dim)]
    ppermute x18 -> x0, starting transfers between devices: 19.8 us -> none  [the longest x9 14.4 us: padded_2(): lax.ppermute(head, axis, [((i + 1) % count, i) for i in range(count)])]
  transfers between devices with their start and end apart: 24 -> 0, of which waited for: 14 -> 0; matrix products, arithmetic and copies ran while one was open for 14% -> 0% of each run, Pallas kernels for 0% -> 0%
where the time goes in v1:
time: 73.4 us; the launch traced here: 73.2 us
  Pallas kernels  64 us (87%)
  local copies, waits for them, and re-layouts  6.87 us (9%)
  between operations  2.35 us (3%)
    pallas_call x1, Pallas kernels, per_device(): pl.pallas_call(functools.partial(kernel, q), out_shape=[jax.ShapeDtypeStr...  64 us
    unnamed x4, local copies, waits for them, and re-layouts  6.87 us

profile of v1, /device:TPU:0, one launch (start us, length us, event | category | flops | bytes accessed | tf_op | source)
XLA Modules:
  0.0 73.2 jit_solution(3124546812479351235)
XLA Ops:
  0.6 64.0 %schwarz_step.1 = (f32[64,64,256]{2,1,0:T(8,128)}, f32[64,64,256]{2,1,0:T(8,128)}, f32[1,1]{1,0:T(1,128)}) custom-call(f32[64,64,256]{2,1,0:T(8,128)} %rs_hbm.1, f32[64,64,256]{2,1,0:T(8,128)} %g_hbm.1, f32[2,256,128]{2,1,0:T(8,128)} %constant.20.clone.refs_0_, f32[16,64]{1,0:T(8,128)} %constant.21.clone.refs_1_, f32[128,256]{1,0:T(8,128)} %constant.22.clone.refs_2_, ...), custom_call_target="tpu_custom_call" | custom-call | tf_op jit(solution)/shard_map/schwarz_step/pallas_call | solution.py:407
  64.6 0.0 copy-start
  64.6 4.8 %copy.18 = f32[64,64,256]{2,1,0:T(8,128)} copy(f32[64,64,256]{2,1,0:T(8,128)} %get-tuple-element.12) | data formatting | bytes 8388608
  69.5 0.0 copy-done
  69.5 2.0 %copy.19 = f32[64,64,256]{2,1,0:T(8,128)} copy(f32[64,64,256]{2,1,0:T(8,128)S(1)} %copy-done) | data formatting | bytes 8388608
Async XLA Ops:
  64.6 4.9 %copy-start = (f32[64,64,256]{2,1,0:T(8,128)S(1)}, f32[64,64,256]{2,1,0:T(8,128)}, u32[]{:S(2)}) copy-start(f32[64,64,256]{2,1,0:T(8,128)} %get-tuple-element.13) | copy-start | bytes 12582916

commit v2 on v1

--- a/solution.py
+++ b/solution.py
@@ -66,15 +66,12 @@
         for j in range(rx):
             myi[:, j, :, :, j, :] = lines.reshape(py, hr, ndev, rk)
         myi = myi.reshape(py * rx * hr, ndev * rx * rk)
-        mzi = np.zeros((pz, lz, self.bz + LANES))
-        for g in range(pz):
-            mzi[g, :, : self.bz] = tz[:, g * cz + up_z]
-            mzi[g, :, self.bz] = tz[:, (g * cz - 1) % lz]
-            mzi[g, :, self.bz + LANES - 1] = tz[:, (g * cz + cz) % lz]
-        spread = (np.arange(self.by)[:, None] // COARSEN == np.arange(hr)[None, :]) * 1.0
+        fine_z = np.arange(self.bz * pz) // COARSEN
+        own, around = tz[:, fine_z], tz[:, np.roll(fine_z, 1)] + tz[:, np.roll(fine_z, -1)]
+        mzi = np.stack([m[:, g * self.bz : (g + 1) * self.bz] for g in range(pz) for m in (own, around)])
         ei = SCREEN + eigen_line(lx)[:, None] + eigen_line(lz)[None, :]
         ey = np.repeat(eigen_line(ly)[:, None, None], lz, axis=2)
-        return [t.astype(np.float32) for t in (mz, pool, my, mx, mxi, myi, mzi, spread, ei, ey)]
+        return [t.astype(np.float32) for t in (mz, pool, my, mx, mxi, myi, mzi, ei, ey)]
 
 
 def dot(a, b):
@@ -83,12 +80,12 @@
 
 def kernel(plan, rs_hbm, g_hbm, *refs):
     q = plan
-    table_hbm = refs[:10]
-    up_hbm, res_hbm, norm_out = refs[10:13]
-    tabs = refs[13:23]
-    mz, pool, my, mx, mxi, myi, mzi, spread, ei, ey = tabs
-    (rs, g, r, u, n, yp, zp, yh, zh, pooled, first, r1, s2, r2, flat, s3, r3, s4, r4, zf, wz, nrm,
-     in_sem, tab_sem, out_sem, face_send, face_recv, a_send, a_recv) = refs[23:]
+    table_hbm = refs[:9]
+    up, n, norm_out = refs[9:12]
+    tabs = refs[12:21]
+    mz, pool, my, mx, mxi, myi, mzi, ei, ey = tabs
+    (rs, g, r, u, yp, zp, yh, zh, pooled, rows16, first, r1, s2, r2, flat, s3, r3, s4, r4, zf, zs, co, nrm,
+     in_sem, tab_sem, face_send, face_recv, a_send, a_recv) = refs[21:]
     ndev, group = q.ndev, q.group
     bx, by, bz = q.bx, q.by, q.bz
     ix, iy, iz = lax.axis_index("gx"), lax.axis_index("gy"), lax.axis_index("gz")
@@ -124,14 +121,21 @@
     row = lax.broadcasted_iota(jnp.int32, (by, LANES), 0)
 
     def pack_plane(x, v, phase, acc):
-        lo, hi = acc
         yp[phase, 0, x] = v[0:1, :]
         yp[phase, 1, x] = v[by - 1 : by, :]
-        lo = jnp.where(lane == x, pltpu.roll(v[:, :LANES], x, 1), lo)
-        hi = jnp.where(lane == x, pltpu.roll(v[:, bz - LANES :], (x + 1) % LANES, 1), hi)
-        return lo, hi
-
-    zero_acc = (jnp.zeros((by, LANES), jnp.float32), jnp.zeros((by, LANES), jnp.float32))
+        acc = pltpu.roll(acc, LANES - 2, 1)
+        return jnp.where(lane == 0, v[:, :LANES], jnp.where(lane == LANES - 1, v[:, bz - LANES :], acc))
+
+    def unpack_start(phase):
+        left, right = zh[phase, 0], zh[phase, 0 if q.pz == 2 else 1]
+        left = pltpu.roll(left, (2 * bx - 1) % LANES, 1)
+        right = pltpu.roll(right, (2 * bx - 3) % LANES, 1)
+        return jnp.where(lane % 2 == 0, left, right)
+
+    def unpack_next(sides):
+        return pltpu.roll(sides, LANES - 2, 1)
+
+    zero_acc = jnp.zeros((by, LANES), jnp.float32)
 
     def face_copies(phase, buf):
         xl, xr = (ix + q.px - 1) % q.px, (ix + 1) % q.px
@@ -142,9 +146,11 @@
             (buf.at[bx], buf.at[0], (xr, iy, iz)),
             (yp.at[phase, 0], yh.at[phase, 1], (ix, yl, iz)),
             (yp.at[phase, 1], yh.at[phase, 0], (ix, yr, iz)),
-            (zp.at[phase, 0], zh.at[phase, 1], (ix, iy, zl)),
-            (zp.at[phase, 1], zh.at[phase, 0], (ix, iy, zr)),
+            (zp.at[phase], zh.at[phase, 0], (ix, iy, zr)),
+            (zp.at[phase], zh.at[phase, 1], (ix, iy, zl)),
         ]
+        if q.pz == 2:
+            moves.pop()
         return [
             pltpu.make_async_remote_copy(
                 src_ref=s, dst_ref=d, send_sem=face_send.at[phase, i], recv_sem=face_recv.at[phase, i],
@@ -153,14 +159,11 @@
             for i, (s, d, dev) in enumerate(moves)
         ]
 
-    def plane_sum(x, buf, phase, ylo, yhi, zadd):
+    def plane_sum(x, buf, phase, sides):
         v = buf[x + 1]
-        zlo = pltpu.roll(zh[phase, 0], (LANES - x) % LANES, 1)
-        zhi = pltpu.roll(zh[phase, 1], LANES - 1 - x, 1)
-        if zadd is not None:
-            zlo, zhi = zlo + zadd, zhi + zadd
+        ylo, yhi = yh[phase, 0, x], yh[phase, 1, x]
         tiles = [v[:, t * LANES : (t + 1) * LANES] for t in range(bz // LANES)]
-        up = [pltpu.roll(t, 1, 1) for t in tiles]
+        shift_up = [pltpu.roll(t, 1, 1) for t in tiles]
         down = [pltpu.roll(t, LANES - 1, 1) for t in tiles]
         out = []
         for t, c in enumerate(tiles):
@@ -168,15 +171,14 @@
             total = buf[x, :, cols] + buf[x + 2, :, cols]
             total += jnp.where(row == 0, ylo[:, cols], pltpu.roll(c, 1, 0))
             total += jnp.where(row == by - 1, yhi[:, cols], pltpu.roll(c, by - 1, 0))
-            total += jnp.where(lane == 0, up[t - 1] if t > 0 else zlo, up[t])
-            total += jnp.where(lane == LANES - 1, down[t + 1] if t + 1 < len(tiles) else zhi, down[t])
+            total += jnp.where(lane == 0, shift_up[t - 1] if t > 0 else sides, shift_up[t])
+            total += jnp.where(lane == LANES - 1, down[t + 1] if t + 1 < len(tiles) else sides, down[t])
             out.append(total)
         return v, jnp.concatenate(out, axis=1)
 
     for c in copies_g:
         c.wait()
-    lo, hi = lax.fori_loop(0, bx, lambda x, acc: pack_plane(x, g[x + 1], 0, acc), zero_acc, unroll=4)
-    zp[0, 0], zp[0, 1] = lo, hi
+    zp[0] = lax.fori_loop(0, bx, lambda x, acc: pack_plane(x, g[x + 1], 0, acc), zero_acc, unroll=8)
     pl.semaphore_wait(barrier, ndev - 1)
     faces0 = face_copies(0, g)
     for c in faces0:
@@ -186,29 +188,31 @@
     for c in faces0:
         c.wait_recv()
 
-    def residual_four(i, acc):
+    def residual_four(i, carry):
+        acc, sides = carry
         total = jnp.zeros((by, bz), jnp.float32)
         for a in range(COARSEN):
             x = i * COARSEN + a
-            v, around = plane_sum(x, g, 0, yh[0, 0, x], yh[0, 1, x], None)
+            v, around = plane_sum(x, g, 0, sides)
+            sides = unpack_next(sides)
             res = rs[x] - (DIAG * v - around)
             r[x + 1] = res
             total += res
             acc = pack_plane(x, res, 1, acc)
         pooled[i] = total
-        return acc
-
-    lo, hi = lax.fori_loop(0, q.cx, residual_four, zero_acc)
-    zp[1, 0], zp[1, 1] = lo, hi
+        return acc, sides
+
+    acc, _ = lax.fori_loop(0, q.cx, residual_four, (zero_acc, unpack_start(0)))
+    zp[1] = acc
     for c in copies_t:
         c.wait()
 
     def fold_rows(i, carry):
-        zf[i, : q.cy, :bz] = dot(pool[...], pooled[i])
+        rows16[i] = dot(pool[...], pooled[i])
         return carry
 
     lax.fori_loop(0, q.cx, fold_rows, 0, unroll=True)
-    cells = zf[: q.cx, : q.cy, :bz].reshape(q.cx * q.cy, bz)
+    cells = rows16[...].reshape(q.cx * q.cy, bz)
     first[...] = dot(cells, mz[iz]).reshape(first.shape)
 
     def spread_out(src, dst, stage, peers, here, device_of, own):
@@ -233,14 +237,19 @@
     for c in faces1:
         c.start()
 
-    def fix_planes(start, stop, acc):
-        def body(x, acc):
-            v, around = plane_sum(x, r, 1, yh[1, 0, x], yh[1, 1, x], None)
-            out = g[x + 1] + (v + around * (1.0 / DIAG)) * (1.0 / DIAG)
-            u[x + 1] = out
-            return pack_plane(x, out, 2, acc)
-
-        return lax.fori_loop(start, stop, body, acc, unroll=2)
+    def fix_planes(start, stop, carry):
+        def body(i, carry):
+            acc, sides = carry
+            for a in range(COARSEN):
+                x = i * COARSEN + a
+                v, around = plane_sum(x, r, 1, sides)
+                sides = unpack_next(sides)
+                out = g[x + 1] + (v + around * (1.0 / DIAG)) * (1.0 / DIAG)
+                u[x + 1] = out
+                acc = pack_plane(x, out, 2, acc)
+            return acc, sides
+
+        return lax.fori_loop(start, stop, body, carry)
 
     all_bytes(r1, group - 1, a_recv.at[0])
     lines = dot(my[...], r1[...].reshape(group * q.rx * q.cy, q.lz))
@@ -249,7 +258,7 @@
     spread_out(s2, r2, 1, ndev, me, coords, s2[me])
     for c in faces1:
         c.wait_recv()
-    acc = fix_planes(0, bx // 2, zero_acc)
+    carry = fix_planes(0, q.cx // 2, (zero_acc, unpack_start(1)))
     all_bytes(r2, ndev - 1, a_recv.at[1])
     for d in range(ndev):
         flat[d * q.rows : (d + 1) * q.rows] = r2[d]
@@ -261,8 +270,7 @@
     for d in range(ndev):
         s3[d] = lines[d * q.rows : (d + 1) * q.rows]
     spread_out(s3, r3, 2, ndev, me, coords, s3[me])
-    lo, hi = fix_planes(bx // 2, bx, acc)
-    zp[2, 0], zp[2, 1] = lo, hi
+    zp[2] = fix_planes(q.cx // 2, q.cx, carry)[0]
     faces2 = face_copies(2, u)
     for c in faces2:
         c.start()
@@ -274,13 +282,13 @@
     def send_lines(k, carry):
         d = (me_p + k) % group
         pltpu.make_async_remote_copy(
-            src_ref=s4.at[d // q.pz], dst_ref=r4.at[pl.ds(me_p * q.rx, q.rx)],
+            src_ref=s4.at[d // q.pz], dst_ref=r4.at[pl.ds(1 + me_p * q.rx, q.rx)],
             send_sem=a_send.at[3], recv_sem=a_recv.at[3], device_id=in_group(d), device_id_type=MESH,
         ).start()
         return carry
 
     lax.fori_loop(1, group, send_lines, 0)
-    r4[pl.ds(me_p * q.rx, q.rx)] = s4[iy]
+    r4[pl.ds(1 + me_p * q.rx, q.rx)] = s4[iy]
 
     def edge(to_x, j, slot, sem):
         def send(d, carry):
@@ -294,55 +302,74 @@
 
     @pl.when(me_p == group - 1)
     def _():
-        edge((ix + 1) % q.px, q.rx - 1, q.cx, 4)
+        edge((ix + 1) % q.px, q.rx - 1, 0, 4)
 
     @pl.when(me_p == 0)
     def _():
         edge((ix + q.px - 1) % q.px, 0, q.cx + 1, 5)
 
+    for c in faces2:
+        c.wait_recv()
+
+    def before_four(i, sides):
+        for a in range(COARSEN):
+            x = i * COARSEN + a
+            v, around = plane_sum(x, u, 2, sides)
+            sides = unpack_next(sides)
+            n[x] = rs[x] - (DIAG * v - around)
+        return sides
+
+    lax.fori_loop(0, q.cx, before_four, unpack_start(2))
+
     all_bytes(r4, (group - 1) * q.rx, a_recv.at[3])
     all_bytes(r4, 1, a_recv.at[4])
     all_bytes(r4, 1, a_recv.at[5])
-    zf[...] = dot(r4[...].reshape((q.cx + 2) * q.hr, q.lz), mzi[iz]).reshape(zf.shape)
-
-    def prolong(i, carry):
-        fine = dot(spread[...], zf[i])
-        wz[i] = fine[:, bz:]
-        for a in range(COARSEN):
-            u[1 + i * COARSEN + a] += fine[:, :bz]
+    lines = r4[...].reshape((q.cx + 2) * q.hr, q.lz)
+    zf[...] = dot(lines, mzi[2 * iz]).reshape(zf.shape)
+    zs[...] = dot(lines[q.hr : -q.hr], mzi[2 * iz + 1]).reshape(zs.shape)
+
+    def coarse_rows(i, carry):
+        c = zf[i + 1]
+        mid = c[: q.cy]
+        co[i, 0] = mid
+        co[i, 1] = (DIAG - 4.0) * mid - zs[i, : q.cy]
+        co[i, 2] = mid - zf[i, : q.cy]
+        co[i, 3] = mid - zf[i + 2, : q.cy]
+        co[i, 4] = mid - jnp.concatenate([c[q.cy : q.cy + 1], c[: q.cy - 1]], axis=0)
+        co[i, 5] = mid - jnp.concatenate([c[1 : q.cy], c[q.cy + 1 : q.cy + 2]], axis=0)
         return carry
 
-    for c in faces2:
-        c.wait_send()
-    lax.fori_loop(0, q.cx, prolong, 0)
-    out_u = pltpu.make_async_copy(u.at[pl.ds(1, bx)], up_hbm, out_sem.at[0])
-    out_u.start()
-    for c in faces2:
-        c.wait_recv()
-    u[0] += dot(spread[...], zf[q.cx])[:, :bz]
-    u[bx + 1] += dot(spread[...], zf[q.cx + 1])[:, :bz]
-
-    out_planes = bx // in_chunks
-    outs_n = []
-    total = jnp.zeros((by, bz), jnp.float32)
-    for c in range(in_chunks):
-
-        def last_four(i, total):
-            ylo, yhi = zf[i, q.cy : q.cy + 1, :bz], zf[i, q.cy + 1 : q.cy + 2, :bz]
+    lax.fori_loop(0, q.cx, coarse_rows, 0, unroll=2)
+
+    sub = lax.broadcasted_iota(jnp.int32, (8, bz), 0)
+    first_half = sub < COARSEN
+
+    def finish(i, total):
+        for t in range(by // 8):
+            def spread(slot):
+                lo = jnp.broadcast_to(co[i, slot, 2 * t : 2 * t + 1], (8, bz))
+                hi = jnp.broadcast_to(co[i, slot, 2 * t + 1 : 2 * t + 2], (8, bz))
+                return jnp.where(first_half, lo, hi)
+
+            ys = slice(8 * t, 8 * t + 8)
+            p = spread(0)
+            flat_part = spread(1)
+            flat_part += jnp.where(sub % COARSEN == 0, spread(4), 0.0)
+            flat_part += jnp.where(sub % COARSEN == COARSEN - 1, spread(5), 0.0)
             for a in range(COARSEN):
                 x = i * COARSEN + a
-                v, around = plane_sum(x, u, 2, yh[2, 0, x] + ylo, yh[2, 1, x] + yhi, wz[i])
-                res = rs[x] - (DIAG * v - around)
-                n[x] = res
+                change = flat_part
+                if a == 0:
+                    change = change + spread(2)
+                if a == COARSEN - 1:
+                    change = change + spread(3)
+                up[x, ys] = u[x + 1, ys] + p
+                res = n[x, ys] - change
+                n[x, ys] = res
                 total += res * res
-            return total
-
-        total = lax.fori_loop(c * q.cx // in_chunks, (c + 1) * q.cx // in_chunks, last_four, total)
-        cp = pltpu.make_async_copy(
-            n.at[pl.ds(c * out_planes, out_planes)], res_hbm.at[pl.ds(c * out_planes, out_planes)], out_sem.at[1 + c]
-        )
-        cp.start()
-        outs_n.append(cp)
+        return total
+
+    total = lax.fori_loop(0, q.cx, finish, jnp.zeros((8, bz), jnp.float32))
 
     line = jnp.sum(total, axis=0, keepdims=True)
     part = line[:, :LANES]
@@ -376,50 +403,47 @@
     def _():
         all_bytes(r4, group, a_send.at[5])
 
-    for c in faces0 + faces1:
+    for c in faces0 + faces1 + faces2:
         c.wait_send()
-    out_u.wait()
-    for cp in outs_n:
-        cp.wait()
 
 
 def per_device(right_side, guess):
     counts = tuple(lax.axis_size(a) for a in ("gx", "gy", "gz"))
     q = Plan(counts, guess.shape)
-    assert q.lz == LANES and q.bx <= LANES and q.bz % LANES == 0
+    assert q.lz == LANES and 2 * q.bx <= LANES and q.bz % LANES == 0 and q.by % 8 == 0
     tables = q.tables()
     f32 = jnp.float32
     bx, by, bz = guess.shape
     vm = lambda *shape: pltpu.VMEM(shape, f32)
     scratch = [vm(*t.shape) for t in tables] + [
-        vm(bx, by, bz), vm(bx + 2, by, bz), vm(bx + 2, by, bz), vm(bx + 2, by, bz), vm(bx, by, bz),
-        vm(3, 2, bx, 1, bz), vm(3, 2, by, LANES), vm(3, 2, bx, 1, bz), vm(3, 2, by, LANES),
-        vm(q.cx, by, bz),
+        vm(bx, by, bz), vm(bx + 2, by, bz), vm(bx + 2, by, bz), vm(bx + 2, by, bz),
+        vm(3, 2, bx, 1, bz), vm(3, by, LANES), vm(3, 2, bx, 1, bz), vm(3, 2, by, LANES),
+        vm(q.cx, by, bz), vm(q.cx, q.cy, bz),
         vm(q.group, q.rx, q.cy, q.lz), vm(q.group, q.rx, q.cy, q.lz),
         vm(q.ndev, q.rows, q.lz), vm(q.ndev, q.rows, q.lz), vm(q.ndev * q.rows, q.lz),
         vm(q.ndev, q.rows, q.lz), vm(q.ndev, q.rows, q.lz),
         vm(q.py, q.rx, q.hr, q.lz), vm(q.cx + 2, q.hr, q.lz),
-        vm(q.cx + 2, q.hr, bz + LANES), vm(q.cx, by, LANES), vm(q.ndev, 1, LANES),
-        pltpu.SemaphoreType.DMA((8,)), pltpu.SemaphoreType.DMA((len(tables),)), pltpu.SemaphoreType.DMA((5,)),
+        vm(q.cx + 2, q.hr, bz), vm(q.cx, q.hr, bz), vm(q.cx, 6, q.cy, bz), vm(q.ndev, 1, LANES),
+        pltpu.SemaphoreType.DMA((8,)), pltpu.SemaphoreType.DMA((len(tables),)),
         pltpu.SemaphoreType.DMA((3, 6)), pltpu.SemaphoreType.DMA((3, 6)),
         pltpu.SemaphoreType.DMA((7,)), pltpu.SemaphoreType.DMA((7,)),
     ]
     updated, new_residual, norm = pl.pallas_call(
         functools.partial(kernel, q),
         out_shape=[
-            jax.ShapeDtypeStruct(guess.shape, f32),
-            jax.ShapeDtypeStruct(guess.shape, f32),
+            pltpu.VMEM(guess.shape, f32),
+            pltpu.VMEM(guess.shape, f32),
             jax.ShapeDtypeStruct((1, 1), f32),
         ],
         in_specs=[pl.BlockSpec(memory_space=pl.ANY)] * (2 + len(tables)),
         out_specs=[
-            pl.BlockSpec(memory_space=pl.ANY),
-            pl.BlockSpec(memory_space=pl.ANY),
+            pl.BlockSpec(memory_space=pltpu.VMEM),
+            pl.BlockSpec(memory_space=pltpu.VMEM),
             pl.BlockSpec(memory_space=pltpu.VMEM),
         ],
         scratch_shapes=scratch,
         compiler_params=pltpu.CompilerParams(
-            collective_id=0, has_side_effects=True, vmem_limit_bytes=60 * 1024 * 1024
+            collective_id=0, has_side_effects=True, vmem_limit_bytes=57100 * 1024
         ),
         name="schwarz_step",
     )(right_side, guess, *[jnp.asarray(t) for t in tables])

time: 73.4 us -> 61.3 us (0.84)
  Pallas kernels: 64 us -> 54.8 us
  local copies, waits for them, and re-layouts: 6.87 us -> 4.03 us
    pallas_call x1, Pallas kernels: 64 us -> 54.8 us  [per_device(): pl.pallas_call(functools.partial(kernel, q), out_shape=[pltpu.VMEM(guess....]
    unnamed x4 -> x2, local copies, waits for them, and re-layouts: 6.87 us -> 4.03 us
where the time goes in v2:
time: 61.3 us; the launch traced here: 61.1 us
  Pallas kernels  54.8 us (89%)
  local copies, waits for them, and re-layouts  4.03 us (7%)
  between operations  2.33 us (4%)
    pallas_call x1, Pallas kernels, per_device(): pl.pallas_call(functools.partial(kernel, q), out_shape=[pltpu.VMEM(guess....  54.8 us
    unnamed x2, local copies, waits for them, and re-layouts  4.03 us

profile of v2, /device:TPU:0, one launch (start us, length us, event | category | flops | bytes accessed | tf_op | source)
XLA Modules:
  0.0 61.1 jit_solution(3631741939619541098)
XLA Ops:
  0.6 54.8 %schwarz_step.1 = (f32[64,64,256]{2,1,0:T(8,128)S(1)}, f32[64,64,256]{2,1,0:T(8,128)S(1)}, f32[1,1]{1,0:T(1,128)}) custom-call(f32[64,64,256]{2,1,0:T(8,128)} %rs_hbm.1, f32[64,64,256]{2,1,0:T(8,128)} %g_hbm.1, f32[2,256,128]{2,1,0:T(8,128)} %constant.18.clone.refs_0_, f32[16,64]{1,0:T(8,128)} %constant.19.clone.refs_1_, f32[128,256]{1,0:T(8,128)} %constant.20.clone.refs_2_, ...), custom_call_target="tpu_custom_call" | custom-call | tf_op jit(solution)/shard_map/schwarz_step/pallas_call | solution.py:431
  55.4 2.0 %copy.17 = f32[64,64,256]{2,1,0:T(8,128)} copy(f32[64,64,256]{2,1,0:T(8,128)S(1)} %get-tuple-element.9) | data formatting | bytes 8388608
  57.4 2.0 %copy.18 = f32[64,64,256]{2,1,0:T(8,128)} copy(f32[64,64,256]{2,1,0:T(8,128)S(1)} %get-tuple-element.10) | data formatting | bytes 8388608

commit v3 on v2

--- a/solution.py
+++ b/solution.py
@@ -92,8 +92,13 @@
     me_p = iy * q.pz + iz
     me = ix * group + me_p
 
-    def coords(lin):
-        return (lin // group, (lin % group) // q.pz, lin % q.pz)
+    def wrapped(i, count):
+        return [i] + [jnp.where(i + d >= count, i + d - count, i + d) for d in range(1, count)]
+
+    xs, ys_, zs_ = wrapped(ix, q.px), wrapped(iy, q.py), wrapped(iz, q.pz)
+    far_first = sorted(range(q.px), key=lambda d: -min(d, q.px - d))
+    group_peers = [(ix, b, c) for b in reversed(ys_) for c in reversed(zs_)][: group - 1]
+    all_peers = [(xs[a], b, c) for a in far_first for b in reversed(ys_) for c in reversed(zs_)][: ndev - 1]
 
     in_chunks = 4
     step = bx // in_chunks
@@ -111,20 +116,23 @@
 
     barrier = pltpu.get_barrier_semaphore()
 
-    def greet(k, carry):
-        pl.semaphore_signal(barrier, inc=1, device_id=coords((me + k) % ndev), device_id_type=MESH)
-        return carry
-
-    lax.fori_loop(1, ndev, greet, 0)
+    for peer in all_peers:
+        pl.semaphore_signal(barrier, inc=1, device_id=peer, device_id_type=MESH)
 
     lane = lax.broadcasted_iota(jnp.int32, (by, LANES), 1)
     row = lax.broadcasted_iota(jnp.int32, (by, LANES), 0)
 
-    def pack_plane(x, v, phase, acc):
+    def pack_plane(x, v, phase, acc, back=0):
         yp[phase, 0, x] = v[0:1, :]
         yp[phase, 1, x] = v[by - 1 : by, :]
-        acc = pltpu.roll(acc, LANES - 2, 1)
-        return jnp.where(lane == 0, v[:, :LANES], jnp.where(lane == LANES - 1, v[:, bz - LANES :], acc))
+        edge = jnp.where(lane == 0, v[:, :LANES], v[:, bz - LANES :])
+        to = (LANES - 2 * back) % LANES
+        if back:
+            edge = pltpu.roll(edge, to, 1)
+        return jnp.where((lane == to) | (lane == (to + LANES - 1) % LANES), edge, acc)
+
+    def pack_next(acc, planes):
+        return pltpu.roll(acc, LANES - 2 * planes, 1)
 
     def unpack_start(phase):
         left, right = zh[phase, 0], zh[phase, 0 if q.pz == 2 else 1]
@@ -132,8 +140,8 @@
         right = pltpu.roll(right, (2 * bx - 3) % LANES, 1)
         return jnp.where(lane % 2 == 0, left, right)
 
-    def unpack_next(sides):
-        return pltpu.roll(sides, LANES - 2, 1)
+    def ahead(sides, planes):
+        return pltpu.roll(sides, LANES - 2 * planes, 1) if planes else sides
 
     zero_acc = jnp.zeros((by, LANES), jnp.float32)
 
@@ -178,7 +186,15 @@
 
     for c in copies_g:
         c.wait()
-    zp[0] = lax.fori_loop(0, bx, lambda x, acc: pack_plane(x, g[x + 1], 0, acc), zero_acc, unroll=8)
+    many = 4 * COARSEN
+
+    def pack_many(i, acc):
+        acc = pack_next(acc, many)
+        for a in range(many):
+            acc = pack_plane(i * many + a, g[i * many + a + 1], 0, acc, many - 1 - a)
+        return acc
+
+    zp[0] = lax.fori_loop(0, bx // many, pack_many, zero_acc)
     pl.semaphore_wait(barrier, ndev - 1)
     faces0 = face_copies(0, g)
     for c in faces0:
@@ -190,17 +206,17 @@
 
     def residual_four(i, carry):
         acc, sides = carry
+        acc = pack_next(acc, COARSEN)
         total = jnp.zeros((by, bz), jnp.float32)
         for a in range(COARSEN):
             x = i * COARSEN + a
-            v, around = plane_sum(x, g, 0, sides)
-            sides = unpack_next(sides)
+            v, around = plane_sum(x, g, 0, ahead(sides, a))
             res = rs[x] - (DIAG * v - around)
             r[x + 1] = res
             total += res
-            acc = pack_plane(x, res, 1, acc)
+            acc = pack_plane(x, res, 1, acc, COARSEN - 1 - a)
         pooled[i] = total
-        return acc, sides
+        return acc, ahead(sides, COARSEN)
 
     acc, _ = lax.fori_loop(0, q.cx, residual_four, (zero_acc, unpack_start(0)))
     zp[1] = acc
@@ -215,24 +231,22 @@
     cells = rows16[...].reshape(q.cx * q.cy, bz)
     first[...] = dot(cells, mz[iz]).reshape(first.shape)
 
-    def spread_out(src, dst, stage, peers, here, device_of, own):
-        def send(k, carry):
-            d = (here + k) % peers
+    def spread_out(src, dst, stage, peers, here, own):
+        for px, py, pz in peers:
+            d = py * q.pz + pz
+            if len(peers) >= group:
+                d = d + px * group
             pltpu.make_async_remote_copy(
                 src_ref=src.at[d], dst_ref=dst.at[here], send_sem=a_send.at[stage], recv_sem=a_recv.at[stage],
-                device_id=device_of(d), device_id_type=MESH,
+                device_id=(px, py, pz), device_id_type=MESH,
             ).start()
-            return carry
-
-        lax.fori_loop(1, peers, send, 0)
         dst[here] = own
 
     def all_bytes(dst, count, sem):
         part = dst.at[pl.ds(0, count)]
         pltpu.make_async_copy(part, part, sem).wait()
 
-    in_group = lambda d: (ix, d // q.pz, d % q.pz)
-    spread_out(first, r1, 0, group, me_p, in_group, first[me_p])
+    spread_out(first, r1, 0, group_peers, me_p, first[me_p])
     faces1 = face_copies(1, r)
     for c in faces1:
         c.start()
@@ -240,14 +254,14 @@
     def fix_planes(start, stop, carry):
         def body(i, carry):
             acc, sides = carry
+            acc = pack_next(acc, COARSEN)
             for a in range(COARSEN):
                 x = i * COARSEN + a
-                v, around = plane_sum(x, r, 1, sides)
-                sides = unpack_next(sides)
+                v, around = plane_sum(x, r, 1, ahead(sides, a))
                 out = g[x + 1] + (v + around * (1.0 / DIAG)) * (1.0 / DIAG)
                 u[x + 1] = out
-                acc = pack_plane(x, out, 2, acc)
-            return acc, sides
+                acc = pack_plane(x, out, 2, acc, COARSEN - 1 - a)
+            return acc, ahead(sides, COARSEN)
 
         return lax.fori_loop(start, stop, body, carry)
 
@@ -255,7 +269,7 @@
     lines = dot(my[...], r1[...].reshape(group * q.rx * q.cy, q.lz))
     for d in range(ndev):
         s2[d] = lines[d * q.rows : (d + 1) * q.rows]
-    spread_out(s2, r2, 1, ndev, me, coords, s2[me])
+    spread_out(s2, r2, 1, all_peers, me, s2[me])
     for c in faces1:
         c.wait_recv()
     carry = fix_planes(0, q.cx // 2, (zero_acc, unpack_start(1)))
@@ -269,7 +283,7 @@
     lines = dot(mxi[...], spec)
     for d in range(ndev):
         s3[d] = lines[d * q.rows : (d + 1) * q.rows]
-    spread_out(s3, r3, 2, ndev, me, coords, s3[me])
+    spread_out(s3, r3, 2, all_peers, me, s3[me])
     zp[2] = fix_planes(q.cx // 2, q.cx, carry)[0]
     faces2 = face_copies(2, u)
     for c in faces2:
@@ -279,15 +293,11 @@
         flat[d * q.rows : (d + 1) * q.rows] = r3[d]
     s4[...] = dot(myi[...], flat[...]).reshape(s4.shape)
 
-    def send_lines(k, carry):
-        d = (me_p + k) % group
+    for peer in group_peers:
         pltpu.make_async_remote_copy(
-            src_ref=s4.at[d // q.pz], dst_ref=r4.at[pl.ds(1 + me_p * q.rx, q.rx)],
-            send_sem=a_send.at[3], recv_sem=a_recv.at[3], device_id=in_group(d), device_id_type=MESH,
+            src_ref=s4.at[peer[1]], dst_ref=r4.at[pl.ds(1 + me_p * q.rx, q.rx)],
+            send_sem=a_send.at[3], recv_sem=a_recv.at[3], device_id=peer, device_id_type=MESH,
         ).start()
-        return carry
-
-    lax.fori_loop(1, group, send_lines, 0)
     r4[pl.ds(1 + me_p * q.rx, q.rx)] = s4[iy]
 
     def edge(to_x, j, slot, sem):
@@ -314,10 +324,9 @@
     def before_four(i, sides):
         for a in range(COARSEN):
             x = i * COARSEN + a
-            v, around = plane_sum(x, u, 2, sides)
-            sides = unpack_next(sides)
+            v, around = plane_sum(x, u, 2, ahead(sides, a))
             n[x] = rs[x] - (DIAG * v - around)
-        return sides
+        return ahead(sides, COARSEN)
 
     lax.fori_loop(0, q.cx, before_four, unpack_start(2))
 
@@ -344,26 +353,24 @@
     sub = lax.broadcasted_iota(jnp.int32, (8, bz), 0)
     first_half = sub < COARSEN
 
+    def spread(i, t, slot):
+        lo = jnp.broadcast_to(co[i, slot, 2 * t : 2 * t + 1], (8, bz))
+        hi = jnp.broadcast_to(co[i, slot, 2 * t + 1 : 2 * t + 2], (8, bz))
+        return jnp.where(first_half, lo, hi)
+
     def finish(i, total):
         for t in range(by // 8):
-            def spread(slot):
-                lo = jnp.broadcast_to(co[i, slot, 2 * t : 2 * t + 1], (8, bz))
-                hi = jnp.broadcast_to(co[i, slot, 2 * t + 1 : 2 * t + 2], (8, bz))
-                return jnp.where(first_half, lo, hi)
-
             ys = slice(8 * t, 8 * t + 8)
-            p = spread(0)
-            flat_part = spread(1)
-            flat_part += jnp.where(sub % COARSEN == 0, spread(4), 0.0)
-            flat_part += jnp.where(sub % COARSEN == COARSEN - 1, spread(5), 0.0)
+            flat_part = spread(i, t, 1)
+            flat_part += jnp.where(sub % COARSEN == 0, spread(i, t, 4), 0.0)
+            flat_part += jnp.where(sub % COARSEN == COARSEN - 1, spread(i, t, 5), 0.0)
             for a in range(COARSEN):
                 x = i * COARSEN + a
                 change = flat_part
                 if a == 0:
-                    change = change + spread(2)
+                    change = change + spread(i, t, 2)
                 if a == COARSEN - 1:
-                    change = change + spread(3)
-                up[x, ys] = u[x + 1, ys] + p
+                    change = change + spread(i, t, 3)
                 res = n[x, ys] - change
                 n[x, ys] = res
                 total += res * res
@@ -377,15 +384,21 @@
         part = part + line[:, t * LANES : (t + 1) * LANES]
     nrm[me] = part
 
-    def send_norm(k, carry):
-        d = (me + k) % ndev
+    for peer in all_peers:
         pltpu.make_async_remote_copy(
             src_ref=nrm.at[me], dst_ref=nrm.at[me], send_sem=a_send.at[6], recv_sem=a_recv.at[6],
-            device_id=coords(d), device_id_type=MESH,
+            device_id=peer, device_id_type=MESH,
         ).start()
+
+    def finish_update(i, carry):
+        for t in range(by // 8):
+            ys = slice(8 * t, 8 * t + 8)
+            p = spread(i, t, 0)
+            for x in range(COARSEN):
+                up[i * COARSEN + x, ys] = u[i * COARSEN + x + 1, ys] + p
         return carry
 
-    lax.fori_loop(1, ndev, send_norm, 0)
+    lax.fori_loop(0, q.cx, finish_update, 0)
     all_bytes(nrm, ndev - 1, a_recv.at[6])
     norm_out[...] = jnp.sqrt(jnp.sum(jnp.sum(nrm[...], axis=0), axis=1, keepdims=True)).reshape(1, 1)
 
@@ -410,7 +423,7 @@
 def per_device(right_side, guess):
     counts = tuple(lax.axis_size(a) for a in ("gx", "gy", "gz"))
     q = Plan(counts, guess.shape)
-    assert q.lz == LANES and 2 * q.bx <= LANES and q.bz % LANES == 0 and q.by % 8 == 0
+    assert q.lz == LANES and 2 * q.bx <= LANES and q.bz % LANES == 0 and q.by % 8 == 0 and q.bx % 16 == 0
     tables = q.tables()
     f32 = jnp.float32
     bx, by, bz = guess.shape

time: 61.3 us -> 58 us (0.946)
  Pallas kernels: 54.8 us -> 51.5 us
    pallas_call x1, Pallas kernels: 54.8 us -> 51.5 us  [per_device(): pl.pallas_call(functools.partial(kernel, q), out_shape=[pltpu.VMEM(guess....]
where the time goes in v3:
time: 58 us; the launch traced here: 57.8 us
  Pallas kernels  51.5 us (89%)
  local copies, waits for them, and re-layouts  4.03 us (7%)
  between operations  2.33 us (4%)
    pallas_call x1, Pallas kernels, per_device(): pl.pallas_call(functools.partial(kernel, q), out_shape=[pltpu.VMEM(guess....  51.5 us
    unnamed x2, local copies, waits for them, and re-layouts  4.03 us

profile of v3, /device:TPU:0, one launch (start us, length us, event | category | flops | bytes accessed | tf_op | source)
XLA Modules:
  0.0 57.8 jit_solution(439464228914031585)
XLA Ops:
  0.6 51.5 %schwarz_step.1 = (f32[64,64,256]{2,1,0:T(8,128)S(1)}, f32[64,64,256]{2,1,0:T(8,128)S(1)}, f32[1,1]{1,0:T(1,128)}) custom-call(f32[64,64,256]{2,1,0:T(8,128)} %rs_hbm.1, f32[64,64,256]{2,1,0:T(8,128)} %g_hbm.1, f32[2,256,128]{2,1,0:T(8,128)} %constant.18.clone.refs_0_, f32[16,64]{1,0:T(8,128)} %constant.19.clone.refs_1_, f32[128,256]{1,0:T(8,128)} %constant.20.clone.refs_2_, ...), custom_call_target="tpu_custom_call" | custom-call | tf_op jit(solution)/shard_map/schwarz_step/pallas_call | solution.py:444
  52.1 2.0 %copy.17 = f32[64,64,256]{2,1,0:T(8,128)} copy(f32[64,64,256]{2,1,0:T(8,128)S(1)} %get-tuple-element.9) | data formatting | bytes 8388608
  54.1 2.0 %copy.18 = f32[64,64,256]{2,1,0:T(8,128)} copy(f32[64,64,256]{2,1,0:T(8,128)S(1)} %get-tuple-element.10) | data formatting | bytes 8388608

commit v4 on v3

--- a/solution.py
+++ b/solution.py
@@ -100,7 +100,7 @@
     group_peers = [(ix, b, c) for b in reversed(ys_) for c in reversed(zs_)][: group - 1]
     all_peers = [(xs[a], b, c) for a in far_first for b in reversed(ys_) for c in reversed(zs_)][: ndev - 1]
 
-    in_chunks = 4
+    in_chunks = min(4, q.bx // 16)
     step = bx // in_chunks
     copies_g = [
         pltpu.make_async_copy(g_hbm.at[pl.ds(c * step, step)], g.at[pl.ds(1 + c * step, step)], in_sem.at[c])
@@ -111,7 +111,7 @@
         for c in range(in_chunks)
     ]
     copies_t = [pltpu.make_async_copy(a, b, tab_sem.at[i]) for i, (a, b) in enumerate(zip(table_hbm, tabs))]
-    for c in copies_g + copies_r + copies_t:
+    for c in copies_g:
         c.start()
 
     barrier = pltpu.get_barrier_semaphore()
@@ -184,17 +184,25 @@
             out.append(total)
         return v, jnp.concatenate(out, axis=1)
 
-    for c in copies_g:
+    many = 16
+
+    def pack_planes(buf, phase, start, stop, acc):
+        def body(i, acc):
+            acc = pack_next(acc, many)
+            for a in range(many):
+                acc = pack_plane(i * many + a, buf[i * many + a + 1], phase, acc, many - 1 - a)
+            return acc
+
+        return lax.fori_loop(start // many, stop // many, body, acc)
+
+    acc = zero_acc
+    for i, c in enumerate(copies_g):
         c.wait()
-    many = 4 * COARSEN
-
-    def pack_many(i, acc):
-        acc = pack_next(acc, many)
-        for a in range(many):
-            acc = pack_plane(i * many + a, g[i * many + a + 1], 0, acc, many - 1 - a)
-        return acc
-
-    zp[0] = lax.fori_loop(0, bx // many, pack_many, zero_acc)
+        if i == in_chunks - 1:
+            for other in copies_r + copies_t:
+                other.start()
+        acc = pack_planes(g, 0, i * step, (i + 1) * step, acc)
+    zp[0] = acc
     pl.semaphore_wait(barrier, ndev - 1)
     faces0 = face_copies(0, g)
     for c in faces0:
@@ -205,8 +213,7 @@
         c.wait_recv()
 
     def residual_four(i, carry):
-        acc, sides = carry
-        acc = pack_next(acc, COARSEN)
+        sides = carry
         total = jnp.zeros((by, bz), jnp.float32)
         for a in range(COARSEN):
             x = i * COARSEN + a
@@ -214,12 +221,10 @@
             res = rs[x] - (DIAG * v - around)
             r[x + 1] = res
             total += res
-            acc = pack_plane(x, res, 1, acc, COARSEN - 1 - a)
         pooled[i] = total
-        return acc, ahead(sides, COARSEN)
-
-    acc, _ = lax.fori_loop(0, q.cx, residual_four, (zero_acc, unpack_start(0)))
-    zp[1] = acc
+        return ahead(sides, COARSEN)
+
+    lax.fori_loop(0, q.cx, residual_four, unpack_start(0))
     for c in copies_t:
         c.wait()
 
@@ -247,23 +252,21 @@
         pltpu.make_async_copy(part, part, sem).wait()
 
     spread_out(first, r1, 0, group_peers, me_p, first[me_p])
+    zp[1] = pack_planes(r, 1, 0, bx, zero_acc)
     faces1 = face_copies(1, r)
     for c in faces1:
         c.start()
 
-    def fix_planes(start, stop, carry):
-        def body(i, carry):
-            acc, sides = carry
-            acc = pack_next(acc, COARSEN)
+    def fix_planes(start, stop, sides):
+        def body(i, sides):
             for a in range(COARSEN):
                 x = i * COARSEN + a
                 v, around = plane_sum(x, r, 1, ahead(sides, a))
                 out = g[x + 1] + (v + around * (1.0 / DIAG)) * (1.0 / DIAG)
                 u[x + 1] = out
-                acc = pack_plane(x, out, 2, acc, COARSEN - 1 - a)
-            return acc, ahead(sides, COARSEN)
-
-        return lax.fori_loop(start, stop, body, carry)
+            return ahead(sides, COARSEN)
+
+        return lax.fori_loop(start, stop, body, sides)
 
     all_bytes(r1, group - 1, a_recv.at[0])
     lines = dot(my[...], r1[...].reshape(group * q.rx * q.cy, q.lz))
@@ -272,7 +275,7 @@
     spread_out(s2, r2, 1, all_peers, me, s2[me])
     for c in faces1:
         c.wait_recv()
-    carry = fix_planes(0, q.cx // 2, (zero_acc, unpack_start(1)))
+    sides = fix_planes(0, q.cx * 7 // 8, unpack_start(1))
     all_bytes(r2, ndev - 1, a_recv.at[1])
     for d in range(ndev):
         flat[d * q.rows : (d + 1) * q.rows] = r2[d]
@@ -284,7 +287,8 @@
     for d in range(ndev):
         s3[d] = lines[d * q.rows : (d + 1) * q.rows]
     spread_out(s3, r3, 2, all_peers, me, s3[me])
-    zp[2] = fix_planes(q.cx // 2, q.cx, carry)[0]
+    fix_planes(q.cx * 7 // 8, q.cx, sides)
+    zp[2] = pack_planes(u, 2, 0, bx, zero_acc)
     faces2 = face_copies(2, u)
     for c in faces2:
         c.start()

time: 58 us -> 51.4 us (0.89)
  Pallas kernels: 51.5 us -> 44.9 us
    pallas_call x1, Pallas kernels: 51.5 us -> 44.9 us  [per_device(): pl.pallas_call(functools.partial(kernel, q), out_shape=[pltpu.VMEM(guess....]
where the time goes in v4:
time: 51.4 us; the launch traced here: 51.3 us
  Pallas kernels  44.9 us (87%)
  local copies, waits for them, and re-layouts  4.03 us (8%)
  between operations  2.33 us (5%)
    pallas_call x1, Pallas kernels, per_device(): pl.pallas_call(functools.partial(kernel, q), out_shape=[pltpu.VMEM(guess....  44.9 us
    unnamed x2, local copies, waits for them, and re-layouts  4.03 us

profile of v4, /device:TPU:0, one launch (start us, length us, event | category | flops | bytes accessed | tf_op | source)
XLA Modules:
  0.0 51.3 jit_solution(16406873025305256207)
XLA Ops:
  0.6 44.9 %schwarz_step.1 = (f32[64,64,256]{2,1,0:T(8,128)S(1)}, f32[64,64,256]{2,1,0:T(8,128)S(1)}, f32[1,1]{1,0:T(1,128)}) custom-call(f32[64,64,256]{2,1,0:T(8,128)} %rs_hbm.1, f32[64,64,256]{2,1,0:T(8,128)} %g_hbm.1, f32[2,256,128]{2,1,0:T(8,128)} %constant.18.clone.refs_0_, f32[16,64]{1,0:T(8,128)} %constant.19.clone.refs_1_, f32[128,256]{1,0:T(8,128)} %constant.20.clone.refs_2_, ...), custom_call_target="tpu_custom_call" | custom-call | tf_op jit(solution)/shard_map/schwarz_step/pallas_call | solution.py:448
  45.6 2.0 %copy.17 = f32[64,64,256]{2,1,0:T(8,128)} copy(f32[64,64,256]{2,1,0:T(8,128)S(1)} %get-tuple-element.9) | data formatting | bytes 8388608
  47.6 2.0 %copy.18 = f32[64,64,256]{2,1,0:T(8,128)} copy(f32[64,64,256]{2,1,0:T(8,128)S(1)} %get-tuple-element.10) | data formatting | bytes 8388608
